TPU v7x, 128 devices: a whole 4x4x4 slice. The times are simulated.
128 devices in a mesh: row: 16 (over x_lo, z, core), col: 8 (over x_hi, y).
Axes of the slice: x: 4 (x_hi: 2, x_lo: 2; x = x_hi * 2 + x_lo), y: 4, z: 4, core: 2. Of those that a mesh axis runs over, the one named last changes fastest.
Arguments:
- psi: bfloat16 [4096, 4096], P(('row', 'col')), may hold values from -6 to 6
- hpsi: bfloat16 [4096, 4096], P(('row', 'col')), may hold values from -0.09375 to 0.09375
- eigvec: bfloat16 [2, 16, 128, 4, 8, 128], P(None, 'row', None, None, 'col'), may hold values from -0.09375 to 0.09375
Outputs:
- correlation_tiles: float32 [2, 16, 128, 4, 8, 128], P(None, 'row', None, None, 'col')
- updated_tiles: float32 [2, 16, 128, 4, 8, 128], P(None, 'row', None, None, 'col')
- diag_part: float32 [16], replicated
- offdiag_part: float32 [16], replicated
- rotated: bfloat16 [4096, 4, 8, 128], P('row', None, 'col')
All inputs are finite; a program needn't handle non-finite values.
Results may differ from a plain program's by a relative error of at most 0.001.
Values may be sent and summed in bfloat16 or wider, within the bound.
A program may use at most 128 MiB of HBM per device.

v0:
```python
import jax
import jax.numpy as jnp
from jax import lax
from jax.sharding import PartitionSpec as P

PB = 16


def in_one_piece(arrays, axis, split_dim, concat_dim, along):
    both = jnp.concatenate(arrays, axis=along)
    whole, at, gathered = (
        lax.all_to_all(both, axis, split_axis=split_dim, concat_axis=concat_dim, tiled=True),
        0,
        [],
    )
    for a in arrays:
        gathered.append(lax.slice_in_dim(whole, at, at + a.shape[along], axis=along))
        at += a.shape[along]
    return tuple(gathered)


def in_one_piece_2(arrays, axis, dim, along):
    both = jnp.concatenate(arrays, axis=along)
    whole, at, gathered = (lax.all_gather(both, axis, axis=dim, tiled=True), 0, [])
    for a in arrays:
        gathered.append(lax.slice_in_dim(whole, at, at + a.shape[along], axis=along))
        at += a.shape[along]
    return tuple(gathered)


def broadcast(array, axis, root):
    return lax.dynamic_index_in_dim(lax.all_gather(array, axis), root, 0, keepdims=False)


def copy_for_each(array, axis):
    length = lax.axis_size(axis)
    return lax.all_to_all(
        jnp.broadcast_to(array[None], (length, *array.shape)), axis, 0, 0, tiled=True
    )


def joined_along(tiles, dim):
    shape = list(tiles.shape[1:])
    shape[dim] *= tiles.shape[0]
    return jnp.moveaxis(tiles, 0, dim).reshape(shape)


def gather_directly(array, axis, dim):
    tiles = copy_for_each(array, axis)
    return joined_along(tiles, dim)


def over_copies(array, axis):
    everything = copy_for_each(array, axis)
    return jnp.sum(everything, axis=0)


def inner(left, right):
    return lax.dot_general(
        left, right, (((0,), (0,)), ((), ())), preferred_element_type=jnp.float32
    )


def on_device(psi, hpsi, eigvec):
    highest = lax.Precision.HIGHEST
    g_rows = psi.shape[0]
    bands = psi.shape[1]
    row_tiles = eigvec.shape[0]
    tile_size = eigvec.shape[2]
    col_tiles = eigvec.shape[3]
    row_count = lax.axis_size("row")
    col_count = lax.axis_size("col")
    row_id = lax.axis_index("row")
    col_id = lax.axis_index("col")
    gvecs = g_rows * row_count * col_count
    row_width = row_tiles * tile_size
    col_width = col_tiles * tile_size
    lifted = (
        psi.reshape(1, g_rows, row_tiles, row_count, tile_size),
        hpsi.reshape(1, g_rows, row_tiles, row_count, tile_size),
    )
    swapped = in_one_piece((lifted[0], lifted[1]), "row", 3, 0, 1)
    joined = in_one_piece_2((swapped[0], swapped[1]), "col", 1, 0)
    psi_rows = joined[0].reshape(gvecs, row_width)
    hpsi_rows = joined[1].reshape(gvecs, row_width)
    lowered = (
        psi.reshape(g_rows, col_tiles, col_count, tile_size),
        hpsi.reshape(g_rows, col_tiles, col_count, tile_size),
    )
    moved = in_one_piece((lowered[0], lowered[1]), "col", 2, 0, 1)
    stacked = in_one_piece_2((moved[0], moved[1]), "row", 0, 1)
    psi_cols = stacked[0].reshape(gvecs, col_width)
    hpsi_cols = stacked[1].reshape(gvecs, col_width)
    reduced = 0.5 * (inner(psi_rows, hpsi_cols) + inner(hpsi_rows, psi_cols))
    correlation = inner(psi_rows, psi_cols) / float(gvecs)
    blocks = reduced.reshape(row_tiles, tile_size, col_tiles, tile_size)
    leading = blocks[:, :, 0, :PB]
    shared = broadcast(leading, "col", 0)
    panel = gather_directly(shared.reshape(row_tiles, 1, tile_size, PB), "row", 1).reshape(
        bands, PB
    )

    def product(vector):
        local_vec = lax.dynamic_index_in_dim(
            vector.reshape(col_tiles, col_count, tile_size), col_id, 1, keepdims=False
        )
        partial_sum = jnp.einsum("atbs,bs->at", blocks, local_vec, precision=highest)
        summed = over_copies(partial_sum, "col")
        result = gather_directly(summed.reshape(row_tiles, 1, tile_size), "row", 1).reshape(bands)
        return result

    positions = jnp.arange(bands)
    slots = jnp.arange(PB)

    def reflect(step, carry):
        vecs, images, diagonal, offdiag = carry
        column = lax.dynamic_index_in_dim(panel, step, 1, keepdims=False)
        head_v = lax.dynamic_index_in_dim(vecs, step, 0, keepdims=False)
        head_w = lax.dynamic_index_in_dim(images, step, 0, keepdims=False)
        column = (
            column
            - jnp.dot(vecs, head_w, precision=highest)
            - jnp.dot(images, head_v, precision=highest)
        )
        pivot = lax.dynamic_index_in_dim(column, step + 1, 0, keepdims=False)
        below = positions > step + 1
        tail = jnp.sum(jnp.where(below, column * column, 0.0))
        length = jnp.sqrt(pivot * pivot + tail)
        beta = jnp.where(pivot >= 0.0, -length, length)
        tau = (beta - pivot) / beta
        vector = jnp.where(
            positions == step + 1, 1.0, jnp.where(below, column / (pivot - beta), 0.0)
        )
        image = product(vector)
        image = image - jnp.dot(vecs, jnp.dot(vector, images, precision=highest), precision=highest)
        image = image - jnp.dot(images, jnp.dot(vector, vecs, precision=highest), precision=highest)
        image = tau * image
        image = image - 0.5 * tau * jnp.dot(image, vector, precision=highest) * vector
        pick = slots == step
        vecs = jnp.where(pick[None, :], vector[:, None], vecs)
        images = jnp.where(pick[None, :], image[:, None], images)
        diagonal = jnp.where(
            pick, lax.dynamic_index_in_dim(column, step, 0, keepdims=False), diagonal
        )
        offdiag = jnp.where(pick, beta, offdiag)
        return (vecs, images, diagonal, offdiag)

    start_state = (
        jnp.zeros((bands, PB), jnp.float32),
        jnp.zeros((bands, PB), jnp.float32),
        jnp.zeros((PB,), jnp.float32),
        jnp.zeros((PB,), jnp.float32),
    )
    vecs, images, diagonal, offdiag = lax.fori_loop(0, PB, reflect, start_state)

    def rows_of(matrix):
        return lax.dynamic_index_in_dim(
            matrix.reshape(row_tiles, row_count, tile_size, PB), row_id, 1, keepdims=False
        ).reshape(row_width, PB)

    def cols_of(matrix):
        return lax.dynamic_index_in_dim(
            matrix.reshape(col_tiles, col_count, tile_size, PB), col_id, 1, keepdims=False
        ).reshape(col_width, PB)

    updated = (
        reduced
        - jnp.dot(rows_of(vecs), cols_of(images).T, precision=highest)
        - jnp.dot(rows_of(images), cols_of(vecs).T, precision=highest)
    )
    flat = eigvec.reshape(row_width, col_width)
    rotated = lax.psum_scatter(
        jnp.dot(psi_rows, flat, preferred_element_type=jnp.float32),
        "row",
        scatter_dimension=0,
        tiled=True,
    )
    tile_shape = (row_tiles, 1, tile_size, col_tiles, 1, tile_size)
    return (
        correlation.reshape(tile_shape),
        updated.reshape(tile_shape),
        diagonal,
        offdiag,
        rotated.astype(jnp.bfloat16).reshape(rotated.shape[0], col_tiles, 1, tile_size),
    )


def solution(mesh):
    return jax.shard_map(
        on_device,
        mesh=mesh,
        in_specs=(
            P(("row", "col"), None),
            P(("row", "col"), None),
            P(None, "row", None, None, "col", None),
        ),
        out_specs=(
            P(None, "row", None, None, "col", None),
            P(None, "row", None, None, "col", None),
            P(),
            P(),
            P("row", None, "col", None),
        ),
        check_vma=False,
    )
```

profile of v0, /device:TPU:1, one launch (start us, length us, event | category | flops | bytes accessed | tf_op | source)
XLA Modules:
  0.0 919.8 jit_solution(17715437989482282004)
XLA Ops:
  9.5 17.2 %all_to_all.71 = bf16[1,64,2,16,128]{4,1,2,0,3:T(8,128)(2,1)S(1)} all-to-all(bf16[1,64,2,16,128]{4,1,2,0,3:T(8,128)(2,1)S(1)} %copy.78), channel_id=1, replica_groups=mesh['row'=16,'col'=8] {'row'}, dimensions={3} | all-to-all | bytes 1048576 | tf_op jit(solution)/shard_map/all_to_all | solution.py:12
  28.1 15.4 %all_to_all.72 = bf16[32,8,8,128]{3,1,0,2:T(8,128)(2,1)} all-to-all(bf16[32,8,8,128]{3,1,0,2:T(8,128)(2,1)S(1)} %copy.81), channel_id=1, replica_groups=mesh['row'=16,'col'=8] {'col'}, dimensions={2} | all-to-all | bytes 1048576 | tf_op jit(solution)/shard_map/all_to_all | solution.py:12
  43.7 54.6 %all-gather.4.cloned.1.call-done = bf16[32,256,2,1,128]{4,0,3,2,1:T(8,128)(2,1)} async-done(((bf16[32,32,2,1,128]{4,0,3,2,1:T(8,128)(2,1)}), bf16[32,256,2,1,128]{4,0,3,2,1:T(8,128)(2,1)}) %all-gather.4.cloned.1.call-update) | async-done | bytes 4194320 | tf_op jit(solution)/shard_map/all_gather | solution.py:24
  121.5 29.7 %all-gather.6.cloned.1.call-done = bf16[4096,8,1,128]{3,1,2,0:T(8,128)(2,1)} async-done(((bf16[256,8,1,128]{3,1,2,0:T(8,128)(2,1)}), bf16[4096,8,1,128]{3,1,2,0:T(8,128)(2,1)}) %all-gather.6.cloned.1.call-update) | async-done | bytes 8388624 | tf_op jit(solution)/shard_map/all_gather | solution.py:24
  151.1 11.5 %fusion.26 = (bf16[4096,4,1,128]{3,1,2,0:T(4,128)(2,1)}, bf16[4096,4,1,128]{3,1,2,0:T(4,128)(2,1)}) fusion(bf16[4096,8,1,128]{3,1,2,0:T(8,128)(2,1)} %all-gather.6.cloned.1.call-done), kind=kLoop, calls=%fused_computation.52 | loop fusion | bytes 16777216 | tf_op jit(solution)/shard_map/slice | solution.py:26
  162.6 7.6 copy.98
  173.8 7.6 copy.97
  186.0 28.7 %all-gather = f32[16,128,1,16]{1,3,2,0:T(8,128)S(1)} all-gather(f32[2,128,1,16]{1,3,2,0:T(8,128)S(1)} %copy.99), channel_id=2, replica_groups=mesh['row'=16,'col'=8] {'col'}, dimensions={0}, use_global_device_ids=true | all-gather | bytes 147456 | tf_op jit(solution)/shard_map/all_gather | solution.py:32
  215.5 10.7 %all-to-all-start.4 = ((f32[16,2,1,128,16]{3,1,4,2,0:T(2,128)}), f32[16,2,1,128,16]{3,1,4,2,0:T(2,128)S(1)}, u32[]{:S(2)}, u32[]{:S(2)}) async-start(f32[16,2,1,128,16]{3,1,4,2,0:T(2,128)} %broadcast_in_dim.157), calls=%async_computation.4 | async-start | bytes 524288 | tf_op jit(solution)/shard_map/all_to_all | solution.py:37
  233.6 673.6 %while.23 = (s32[]{:T(128)}, f32[4096,16]{1,0:T(8,128)}, f32[4096,16]{1,0:T(8,128)}, f32[16]{0:T(128)S(1)}, f32[16]{0:T(128)S(1)}, /*index=5*/f32[4096,16]{0,1:T...) while((s32[]{:T(128)}, f32[4096,16]{1,0:T(8,128)}, ...), condition=%wide.region_3.4_spmd.clone.clone, body=%wide.region_0.3_spmd.clone.clone.sunk | while | flops 6690686 | bytes 10534969 | solution.py:154
  242.8 5.9 all-to-all-start
  262.8 5.2 all-to-all-done.1
  284.5 7.5 all-to-all-start
  305.5 5.2 all-to-all-done.1
  327.3 6.9 all-to-all-start
  347.8 5.2 all-to-all-done.1
  369.5 6.9 all-to-all-start
  390.0 5.2 all-to-all-done.1
  411.8 6.9 all-to-all-start
  432.2 5.2 all-to-all-done.1
  454.0 6.9 all-to-all-start
  474.5 5.2 all-to-all-done.1
  496.2 6.9 all-to-all-start
  538.5 6.9 all-to-all-start
  580.7 6.9 all-to-all-start
  622.9 6.9 all-to-all-start
  665.2 6.9 all-to-all-start
  707.4 6.9 all-to-all-start
  749.6 6.9 all-to-all-start
  791.9 6.9 all-to-all-start
  834.1 6.9 all-to-all-start
  876.4 6.9 all-to-all-start
  (526 shorter events, 512.7 us)
Async XLA Ops:
  7.2 91.1 %all-gather.4.cloned.1.call-start = ((), (), s32[]{:S(2)}) async-start(), calls=%async_computation.6 | async-start | bytes 4718592 | tf_op jit(solution)/shard_map/all_gather | solution.py:24
  28.0 123.2 %all-gather.6.cloned.1.call-start = ((), (), s32[]{:S(2)}) async-start(), calls=%async_computation.7 | async-start | bytes 8912896 | tf_op jit(solution)/shard_map/all_gather | solution.py:24
  43.6 867.8 %reduce-scatter.2.cloned.1.call-start = ((), (), s32[]{:S(2)}) async-start(), calls=%async_computation.8 | async-start | bytes 8912896 | tf_op jit(solution)/shard_map/reduce_scatter | solution.py:172
  215.5 17.9 %all-to-all-start.4 = ((f32[16,2,1,128,16]{3,1,4,2,0:T(2,128)}), f32[16,2,1,128,16]{3,1,4,2,0:T(2,128)S(1)}, u32[]{:S(2)}, u32[]{:S(2)}) async-start(f32[16,2,1,128,16]{3,1,4,2,0:T(2,128)} %broadcast_in_dim.157), calls=%async_computation.4 | async-start | bytes 524288 | tf_op jit(solution)/shard_map/all_to_all | solution.py:37
  242.8 14.2 %all-to-all-start = ((f32[8,2,128]{2,1,0:T(2,128)}), f32[8,2,128]{2,1,0:T(2,128)S(1)}, u32[]{:S(2)}, u32[]{:S(2)}) async-start(f32[8,2,128]{2,1,0:T(2,128)} %broadcast_in_dim.225), calls=%async_computation | async-start | bytes 16384 | tf_op jit(solution)/shard_map/while/body/eval_jaxpr/all_to_all | solution.py:37
  257.7 10.3 %all-to-all-start.1 = ((f32[16,2,1,128]{3,1,2,0:T(2,128)}), f32[16,2,1,128]{3,1,2,0:T(2,128)S(1)}, u32[]{:S(2)}, u32[]{:S(2)}) async-start(f32[16,2,1,128]{3,1,2,0:T(2,128)} %broadcast_in_dim.226), calls=%async_computation.1 | async-start | bytes 32768 | tf_op jit(solution)/shard_map/while/body/eval_jaxpr/all_to_all | solution.py:37
  284.5 15.8 %all-to-all-start = ((f32[8,2,128]{2,1,0:T(2,128)}), f32[8,2,128]{2,1,0:T(2,128)S(1)}, u32[]{:S(2)}, u32[]{:S(2)}) async-start(f32[8,2,128]{2,1,0:T(2,128)} %broadcast_in_dim.225), calls=%async_computation | async-start | bytes 16384 | tf_op jit(solution)/shard_map/while/body/eval_jaxpr/all_to_all | solution.py:37
  301.0 9.8 %all-to-all-start.1 = ((f32[16,2,1,128]{3,1,2,0:T(2,128)}), f32[16,2,1,128]{3,1,2,0:T(2,128)S(1)}, u32[]{:S(2)}, u32[]{:S(2)}) async-start(f32[16,2,1,128]{3,1,2,0:T(2,128)} %broadcast_in_dim.226), calls=%async_computation.1 | async-start | bytes 32768 | tf_op jit(solution)/shard_map/while/body/eval_jaxpr/all_to_all | solution.py:37
  327.3 15.2 %all-to-all-start = ((f32[8,2,128]{2,1,0:T(2,128)}), f32[8,2,128]{2,1,0:T(2,128)S(1)}, u32[]{:S(2)}, u32[]{:S(2)}) async-start(f32[8,2,128]{2,1,0:T(2,128)} %broadcast_in_dim.225), calls=%async_computation | async-start | bytes 16384 | tf_op jit(solution)/shard_map/while/body/eval_jaxpr/all_to_all | solution.py:37
  343.2 9.8 %all-to-all-start.1 = ((f32[16,2,1,128]{3,1,2,0:T(2,128)}), f32[16,2,1,128]{3,1,2,0:T(2,128)S(1)}, u32[]{:S(2)}, u32[]{:S(2)}) async-start(f32[16,2,1,128]{3,1,2,0:T(2,128)} %broadcast_in_dim.226), calls=%async_computation.1 | async-start | bytes 32768 | tf_op jit(solution)/shard_map/while/body/eval_jaxpr/all_to_all | solution.py:37
  369.5 15.2 %all-to-all-start = ((f32[8,2,128]{2,1,0:T(2,128)}), f32[8,2,128]{2,1,0:T(2,128)S(1)}, u32[]{:S(2)}, u32[]{:S(2)}) async-start(f32[8,2,128]{2,1,0:T(2,128)} %broadcast_in_dim.225), calls=%async_computation | async-start | bytes 16384 | tf_op jit(solution)/shard_map/while/body/eval_jaxpr/all_to_all | solution.py:37
  385.4 9.8 %all-to-all-start.1 = ((f32[16,2,1,128]{3,1,2,0:T(2,128)}), f32[16,2,1,128]{3,1,2,0:T(2,128)S(1)}, u32[]{:S(2)}, u32[]{:S(2)}) async-start(f32[16,2,1,128]{3,1,2,0:T(2,128)} %broadcast_in_dim.226), calls=%async_computation.1 | async-start | bytes 32768 | tf_op jit(solution)/shard_map/while/body/eval_jaxpr/all_to_all | solution.py:37
  411.8 15.2 %all-to-all-start = ((f32[8,2,128]{2,1,0:T(2,128)}), f32[8,2,128]{2,1,0:T(2,128)S(1)}, u32[]{:S(2)}, u32[]{:S(2)}) async-start(f32[8,2,128]{2,1,0:T(2,128)} %broadcast_in_dim.225), calls=%async_computation | async-start | bytes 16384 | tf_op jit(solution)/shard_map/while/body/eval_jaxpr/all_to_all | solution.py:37
  427.7 9.8 %all-to-all-start.1 = ((f32[16,2,1,128]{3,1,2,0:T(2,128)}), f32[16,2,1,128]{3,1,2,0:T(2,128)S(1)}, u32[]{:S(2)}, u32[]{:S(2)}) async-start(f32[16,2,1,128]{3,1,2,0:T(2,128)} %broadcast_in_dim.226), calls=%async_computation.1 | async-start | bytes 32768 | tf_op jit(solution)/shard_map/while/body/eval_jaxpr/all_to_all | solution.py:37
  454.0 15.2 %all-to-all-start = ((f32[8,2,128]{2,1,0:T(2,128)}), f32[8,2,128]{2,1,0:T(2,128)S(1)}, u32[]{:S(2)}, u32[]{:S(2)}) async-start(f32[8,2,128]{2,1,0:T(2,128)} %broadcast_in_dim.225), calls=%async_computation | async-start | bytes 16384 | tf_op jit(solution)/shard_map/while/body/eval_jaxpr/all_to_all | solution.py:37
  469.9 9.8 %all-to-all-start.1 = ((f32[16,2,1,128]{3,1,2,0:T(2,128)}), f32[16,2,1,128]{3,1,2,0:T(2,128)S(1)}, u32[]{:S(2)}, u32[]{:S(2)}) async-start(f32[16,2,1,128]{3,1,2,0:T(2,128)} %broadcast_in_dim.226), calls=%async_computation.1 | async-start | bytes 32768 | tf_op jit(solution)/shard_map/while/body/eval_jaxpr/all_to_all | solution.py:37
  496.2 15.2 %all-to-all-start = ((f32[8,2,128]{2,1,0:T(2,128)}), f32[8,2,128]{2,1,0:T(2,128)S(1)}, u32[]{:S(2)}, u32[]{:S(2)}) async-start(f32[8,2,128]{2,1,0:T(2,128)} %broadcast_in_dim.225), calls=%async_computation | async-start | bytes 16384 | tf_op jit(solution)/shard_map/while/body/eval_jaxpr/all_to_all | solution.py:37
  512.1 9.8 %all-to-all-start.1 = ((f32[16,2,1,128]{3,1,2,0:T(2,128)}), f32[16,2,1,128]{3,1,2,0:T(2,128)S(1)}, u32[]{:S(2)}, u32[]{:S(2)}) async-start(f32[16,2,1,128]{3,1,2,0:T(2,128)} %broadcast_in_dim.226), calls=%async_computation.1 | async-start | bytes 32768 | tf_op jit(solution)/shard_map/while/body/eval_jaxpr/all_to_all | solution.py:37
  538.5 15.2 %all-to-all-start = ((f32[8,2,128]{2,1,0:T(2,128)}), f32[8,2,128]{2,1,0:T(2,128)S(1)}, u32[]{:S(2)}, u32[]{:S(2)}) async-start(f32[8,2,128]{2,1,0:T(2,128)} %broadcast_in_dim.225), calls=%async_computation | async-start | bytes 16384 | tf_op jit(solution)/shard_map/while/body/eval_jaxpr/all_to_all | solution.py:37
  554.4 9.8 %all-to-all-start.1 = ((f32[16,2,1,128]{3,1,2,0:T(2,128)}), f32[16,2,1,128]{3,1,2,0:T(2,128)S(1)}, u32[]{:S(2)}, u32[]{:S(2)}) async-start(f32[16,2,1,128]{3,1,2,0:T(2,128)} %broadcast_in_dim.226), calls=%async_computation.1 | async-start | bytes 32768 | tf_op jit(solution)/shard_map/while/body/eval_jaxpr/all_to_all | solution.py:37
  580.7 15.2 %all-to-all-start = ((f32[8,2,128]{2,1,0:T(2,128)}), f32[8,2,128]{2,1,0:T(2,128)S(1)}, u32[]{:S(2)}, u32[]{:S(2)}) async-start(f32[8,2,128]{2,1,0:T(2,128)} %broadcast_in_dim.225), calls=%async_computation | async-start | bytes 16384 | tf_op jit(solution)/shard_map/while/body/eval_jaxpr/all_to_all | solution.py:37
  596.6 9.8 %all-to-all-start.1 = ((f32[16,2,1,128]{3,1,2,0:T(2,128)}), f32[16,2,1,128]{3,1,2,0:T(2,128)S(1)}, u32[]{:S(2)}, u32[]{:S(2)}) async-start(f32[16,2,1,128]{3,1,2,0:T(2,128)} %broadcast_in_dim.226), calls=%async_computation.1 | async-start | bytes 32768 | tf_op jit(solution)/shard_map/while/body/eval_jaxpr/all_to_all | solution.py:37
  622.9 15.2 %all-to-all-start = ((f32[8,2,128]{2,1,0:T(2,128)}), f32[8,2,128]{2,1,0:T(2,128)S(1)}, u32[]{:S(2)}, u32[]{:S(2)}) async-start(f32[8,2,128]{2,1,0:T(2,128)} %broadcast_in_dim.225), calls=%async_computation | async-start | bytes 16384 | tf_op jit(solution)/shard_map/while/body/eval_jaxpr/all_to_all | solution.py:37
  638.8 9.8 %all-to-all-start.1 = ((f32[16,2,1,128]{3,1,2,0:T(2,128)}), f32[16,2,1,128]{3,1,2,0:T(2,128)S(1)}, u32[]{:S(2)}, u32[]{:S(2)}) async-start(f32[16,2,1,128]{3,1,2,0:T(2,128)} %broadcast_in_dim.226), calls=%async_computation.1 | async-start | bytes 32768 | tf_op jit(solution)/shard_map/while/body/eval_jaxpr/all_to_all | solution.py:37
  665.2 15.2 %all-to-all-start = ((f32[8,2,128]{2,1,0:T(2,128)}), f32[8,2,128]{2,1,0:T(2,128)S(1)}, u32[]{:S(2)}, u32[]{:S(2)}) async-start(f32[8,2,128]{2,1,0:T(2,128)} %broadcast_in_dim.225), calls=%async_computation | async-start | bytes 16384 | tf_op jit(solution)/shard_map/while/body/eval_jaxpr/all_to_all | solution.py:37
  681.1 9.8 %all-to-all-start.1 = ((f32[16,2,1,128]{3,1,2,0:T(2,128)}), f32[16,2,1,128]{3,1,2,0:T(2,128)S(1)}, u32[]{:S(2)}, u32[]{:S(2)}) async-start(f32[16,2,1,128]{3,1,2,0:T(2,128)} %broadcast_in_dim.226), calls=%async_computation.1 | async-start | bytes 32768 | tf_op jit(solution)/shard_map/while/body/eval_jaxpr/all_to_all | solution.py:37
  707.4 15.2 %all-to-all-start = ((f32[8,2,128]{2,1,0:T(2,128)}), f32[8,2,128]{2,1,0:T(2,128)S(1)}, u32[]{:S(2)}, u32[]{:S(2)}) async-start(f32[8,2,128]{2,1,0:T(2,128)} %broadcast_in_dim.225), calls=%async_computation | async-start | bytes 16384 | tf_op jit(solution)/shard_map/while/body/eval_jaxpr/all_to_all | solution.py:37
  723.3 9.8 %all-to-all-start.1 = ((f32[16,2,1,128]{3,1,2,0:T(2,128)}), f32[16,2,1,128]{3,1,2,0:T(2,128)S(1)}, u32[]{:S(2)}, u32[]{:S(2)}) async-start(f32[16,2,1,128]{3,1,2,0:T(2,128)} %broadcast_in_dim.226), calls=%async_computation.1 | async-start | bytes 32768 | tf_op jit(solution)/shard_map/while/body/eval_jaxpr/all_to_all | solution.py:37
  749.6 15.2 %all-to-all-start = ((f32[8,2,128]{2,1,0:T(2,128)}), f32[8,2,128]{2,1,0:T(2,128)S(1)}, u32[]{:S(2)}, u32[]{:S(2)}) async-start(f32[8,2,128]{2,1,0:T(2,128)} %broadcast_in_dim.225), calls=%async_computation | async-start | bytes 16384 | tf_op jit(solution)/shard_map/while/body/eval_jaxpr/all_to_all | solution.py:37
  791.9 15.2 %all-to-all-start = ((f32[8,2,128]{2,1,0:T(2,128)}), f32[8,2,128]{2,1,0:T(2,128)S(1)}, u32[]{:S(2)}, u32[]{:S(2)}) async-start(f32[8,2,128]{2,1,0:T(2,128)} %broadcast_in_dim.225), calls=%async_computation | async-start | bytes 16384 | tf_op jit(solution)/shard_map/while/body/eval_jaxpr/all_to_all | solution.py:37
  834.1 15.2 %all-to-all-start = ((f32[8,2,128]{2,1,0:T(2,128)}), f32[8,2,128]{2,1,0:T(2,128)S(1)}, u32[]{:S(2)}, u32[]{:S(2)}) async-start(f32[8,2,128]{2,1,0:T(2,128)} %broadcast_in_dim.225), calls=%async_computation | async-start | bytes 16384 | tf_op jit(solution)/shard_map/while/body/eval_jaxpr/all_to_all | solution.py:37
  876.4 15.2 %all-to-all-start = ((f32[8,2,128]{2,1,0:T(2,128)}), f32[8,2,128]{2,1,0:T(2,128)S(1)}, u32[]{:S(2)}, u32[]{:S(2)}) async-start(f32[8,2,128]{2,1,0:T(2,128)} %broadcast_in_dim.225), calls=%async_computation | async-start | bytes 16384 | tf_op jit(solution)/shard_map/while/body/eval_jaxpr/all_to_all | solution.py:37
  (39 other events, 141.5 us)
Sparse Core Ops, SparseCore 0:
  28.1 70.1 all-gather.3
  100.0 51.1 all-gather.5
  153.5 73.0 reduce-scatter.1
where the time goes:
time: 924 us; the launch traced here: 920 us
  matrix products  205 us (22%)
  starting transfers between devices  185 us (20%)
  waiting for transfers between devices  169 us (18%)
  other arithmetic  131 us (14%)
  local copies, waits for them, and re-layouts  85.7 us (9%)
  loops' own time  68.4 us (7%)
  blocking collectives  61.3 us (7%)
  between operations  14 us (2%)
    all_to_all x33, starting transfers between devices, copy_for_each(): lax.all_to_all(jnp.broadcast_to(array[None], (length, *array.shape)), axi...  185 us
    all_to_all x33, waiting for transfers between devices, copy_for_each(): lax.all_to_all(jnp.broadcast_to(array[None], (length, *array.shape)), axi...  84.9 us
    all_gather x2, waiting for transfers between devices, in_one_piece_2(): lax.all_gather(both, axis, axis=dim, tiled=True)  84.3 us
    another operation x1, loops' own time, on_device(): vecs, images, diagonal, offdiag = lax.fori_loop(0, PB, reflect, start_state)  68.4 us
    select_n x16, other arithmetic, reflect(): images = jnp.where(pick[None, :], image[:, None], images)  61 us
    dot_general x16, matrix products, reflect(): jnp.dot(vector, images, precision=highest)  45.5 us
    while x16, other arithmetic  37.7 us
    all_to_all x2, blocking collectives, in_one_piece(): lax.all_to_all(both, axis, split_axis=split_dim, concat_axis=concat_dim,...  32.6 us
  transfers between devices with their start and end apart: 36, of which 19 were waited for; matrix products, arithmetic and copies ran while one was open for 45% of the time, Pallas kernels for 0%

commit v1 on v0

v1 whole, which is shorter than its diff:
```python
import jax
import jax.numpy as jnp
from jax import lax
from jax.experimental import pallas as pl
from jax.experimental.pallas import tpu as pltpu
from jax.sharding import PartitionSpec as P

PB = 16
MESH = pl.DeviceIdType.MESH


def in_one_piece(arrays, axis, split_dim, concat_dim, along):
    both = jnp.concatenate(arrays, axis=along)
    whole, at, gathered = (
        lax.all_to_all(both, axis, split_axis=split_dim, concat_axis=concat_dim, tiled=True),
        0,
        [],
    )
    for a in arrays:
        gathered.append(lax.slice_in_dim(whole, at, at + a.shape[along], axis=along))
        at += a.shape[along]
    return tuple(gathered)


def in_one_piece_2(arrays, axis, dim, along):
    both = jnp.concatenate(arrays, axis=along)
    whole, at, gathered = (lax.all_gather(both, axis, axis=dim, tiled=True), 0, [])
    for a in arrays:
        gathered.append(lax.slice_in_dim(whole, at, at + a.shape[along], axis=along))
        at += a.shape[along]
    return tuple(gathered)


def inner(left, right):
    return lax.dot_general(
        left, right, (((0,), (0,)), ((), ())), preferred_element_type=jnp.float32
    )


def split_three(x):
    high = x.astype(jnp.bfloat16)
    rest = x - high.astype(jnp.float32)
    mid = rest.astype(jnp.bfloat16)
    low = (rest - mid.astype(jnp.float32)).astype(jnp.bfloat16)
    return high, mid, low


def panel_kernel(
    a_ref,
    updated_ref,
    diag_ref,
    off_ref,
    panel_out,
    panel_in,
    panel,
    vecs,
    images,
    vec,
    lanes_sum,
    parts_out,
    parts_in,
    whole,
    send_sem,
    panel_sem,
    parts_sem,
):
    rows = lax.axis_size("row")
    cols = lax.axis_size("col")
    row = lax.axis_index("row")
    col = lax.axis_index("col")
    height = a_ref.shape[1]
    tile = 128
    blocks = a_ref.shape[2] // tile
    halves = height // tile
    tiles = rows * halves
    order = sorted(range(1, rows), key=lambda d: -min(d, rows - d))
    peers = [{"row": lax.rem(row + d, rows), "col": col} for d in order]
    barrier = pltpu.get_barrier_semaphore()
    for peer in peers:
        pl.semaphore_signal(barrier, inc=1, device_id=peer, device_id_type=MESH)
    pl.semaphore_wait(barrier, rows - 1)

    def to_peers(source, target, recv):
        for peer in peers:
            pltpu.make_async_remote_copy(
                src_ref=source,
                dst_ref=target,
                send_sem=send_sem,
                recv_sem=recv,
                device_id=peer,
                device_id_type=MESH,
            ).start()

    for half in range(halves):
        first = a_ref[0, half * tile : (half + 1) * tile, 0:tile]
        panel_out[:, half, :] = jnp.transpose(first)[0:PB, :]
    to_peers(panel_out, panel_in.at[row], panel_sem)
    panel_in[row] = panel_out[...]
    vecs[...] = jnp.zeros_like(vecs)
    images[...] = jnp.zeros_like(images)
    spot = lax.broadcasted_iota(jnp.int32, (tiles, tile), 0)
    lane = lax.broadcasted_iota(jnp.int32, (tiles, tile), 1)
    positions = ((spot % halves) * rows + spot // halves) * tile + lane
    slot = lax.broadcasted_iota(jnp.int32, (8, tile), 1)
    others = panel_in.at[pl.ds(0, rows - 1)]
    pltpu.make_async_copy(others, others, panel_sem).wait()
    for r in range(rows):
        panel[:, r * halves : (r + 1) * halves, :] = panel_in[r]

    def total(x):
        return jnp.sum(x, axis=(0, 1), keepdims=True)

    def totals(x):
        return jnp.sum(x, axis=(1, 2), keepdims=True)

    def reflector(column, step):
        at = total(jnp.where(positions == step, column, 0.0))
        pivot = total(jnp.where(positions == step + 1, column, 0.0))
        below = positions > step + 1
        tail = total(jnp.where(below, column * column, 0.0))
        length = jnp.sqrt(pivot * pivot + tail)
        beta = jnp.where(pivot >= 0.0, -length, length)
        tau = (beta - pivot) / beta
        vector = jnp.where(
            positions == step + 1, 1.0, jnp.where(below, column / (pivot - beta), 0.0)
        )
        return at, beta, tau, vector

    def advance(step, carry):
        column, diagonal, offdiag = carry
        at, beta, tau, vector = reflector(column, step)
        diagonal = jnp.where(slot == step, at, diagonal)
        offdiag = jnp.where(slot == step, beta, offdiag)
        vec[...] = vector
        spread = [jnp.broadcast_to(vec[e : e + 1, :], (8, tile)) for e in range(tiles)]

        def band(group, _):
            at_rows = pl.ds(pl.multiple_of(group * 8, 8), 8)
            sums = [jnp.zeros((8, tile), jnp.float32) for _ in range(4)]
            for e in range(tiles):
                t = (e % halves) * rows + e // halves
                b = t // cols
                block = a_ref[t % cols, at_rows, b * tile : (b + 1) * tile]
                sums[e % 4] = sums[e % 4] + block * spread[e]
            lanes_sum[at_rows, :] = (sums[0] + sums[1]) + (sums[2] + sums[3])
            return 0

        lax.fori_loop(0, height // 8, band, 0)
        ones = jnp.ones((16, tile), jnp.bfloat16)
        product = jnp.zeros((16, height), jnp.float32)
        for piece in split_three(lanes_sum[...]):
            product = product + lax.dot_general(
                ones, piece, (((1,), (1,)), ((), ())), preferred_element_type=jnp.float32
            )
        for half in range(halves):
            parts_out[step, half : half + 1, :] = product[0:1, half * tile : (half + 1) * tile]
        to_peers(parts_out.at[step], parts_in.at[step, row], parts_sem.at[step])
        parts_in[step, row] = parts_out[step]
        by_vecs = totals(vecs[...] * vector[None])
        by_images = totals(images[...] * vector[None])
        known = jnp.sum(vecs[...] * by_images + images[...] * by_vecs, axis=0)
        following = jnp.minimum(step + 1, PB - 1)
        here = positions == following
        head_v = totals(jnp.where(here[None], vecs[...], 0.0))
        head_w = totals(jnp.where(here[None], images[...], 0.0))
        ahead = panel[following] - jnp.sum(vecs[...] * head_w + images[...] * head_v, axis=0)
        vecs[step] = vector
        rest = parts_in.at[step, pl.ds(0, rows - 1)]
        pltpu.make_async_copy(rest, rest, parts_sem.at[step]).wait()
        for r in range(rows):
            whole[r * halves : (r + 1) * halves, :] = parts_in[step, r]
        image = tau * (whole[...] - known)
        image = image - 0.5 * tau * total(image * vector) * vector
        images[step] = image
        lead_v = total(jnp.where(here, vector, 0.0))
        lead_w = total(jnp.where(here, image, 0.0))
        column = ahead - vector * lead_w - image * lead_v
        return column, diagonal, offdiag

    nothing = jnp.zeros((8, tile), jnp.float32)
    _, diagonal, offdiag = lax.fori_loop(0, PB, advance, (panel[0], nothing, nothing))
    diag_ref[...] = diagonal
    off_ref[...] = offdiag
    left_v = [vecs[:, pl.ds(halves * row + h, 1), :].reshape(PB, tile) for h in range(halves)]
    left_w = [images[:, pl.ds(halves * row + h, 1), :].reshape(PB, tile) for h in range(halves)]
    for b in range(blocks):
        t = b * cols + col
        e = (t % rows) * halves + t // rows
        right_v = vecs[:, pl.ds(e, 1), :].reshape(PB, tile)
        right_w = images[:, pl.ds(e, 1), :].reshape(PB, tile)
        for h in range(halves):
            change = lax.dot_general(
                jnp.concatenate([left_v[h], left_w[h]], axis=0),
                jnp.concatenate([right_w, right_v], axis=0),
                (((0,), (0,)), ((), ())),
                precision=lax.Precision.HIGHEST,
                preferred_element_type=jnp.float32,
            )
            block = a_ref[col, h * tile : (h + 1) * tile, b * tile : (b + 1) * tile]
            updated_ref[pl.ds(h * tile * blocks + b, tile, stride=blocks), :] = block - change

    def drain(_, carry):
        pltpu.make_async_copy(parts_out.at[0], parts_out.at[0], send_sem).wait()
        return carry

    for _ in peers:
        pltpu.make_async_copy(panel_out, panel_out, send_sem).wait()
    lax.fori_loop(0, PB * (rows - 1), drain, 0)


def reduce_panel(a_rows, rows):
    cols, height, width = a_rows.shape
    tile = 128
    halves = height // tile
    tiles = rows * halves
    vmem = pl.BlockSpec(memory_space=pltpu.VMEM)
    return pl.pallas_call(
        panel_kernel,
        out_shape=(
            jax.ShapeDtypeStruct((height * width // tile, tile), jnp.float32),
            jax.ShapeDtypeStruct((8, tile), jnp.float32),
            jax.ShapeDtypeStruct((8, tile), jnp.float32),
        ),
        in_specs=[vmem],
        out_specs=(vmem, vmem, vmem),
        scratch_shapes=[
            pltpu.VMEM((PB, halves, tile), jnp.float32),
            pltpu.VMEM((rows, PB, halves, tile), jnp.float32),
            pltpu.VMEM((PB, tiles, tile), jnp.float32),
            pltpu.VMEM((PB, tiles, tile), jnp.float32),
            pltpu.VMEM((PB, tiles, tile), jnp.float32),
            pltpu.VMEM((tiles, tile), jnp.float32),
            pltpu.VMEM((height, tile), jnp.float32),
            pltpu.VMEM((PB, halves, tile), jnp.float32),
            pltpu.VMEM((PB, rows, halves, tile), jnp.float32),
            pltpu.VMEM((tiles, tile), jnp.float32),
            pltpu.SemaphoreType.DMA,
            pltpu.SemaphoreType.DMA,
            pltpu.SemaphoreType.DMA((PB,)),
        ],
        compiler_params=pltpu.CompilerParams(
            collective_id=0, has_side_effects=True, vmem_limit_bytes=48 * 1024 * 1024
        ),
        name="panel",
    )(a_rows)


def on_device(psi, hpsi, eigvec):
    g_rows = psi.shape[0]
    row_tiles = eigvec.shape[0]
    tile_size = eigvec.shape[2]
    col_tiles = eigvec.shape[3]
    row_count = lax.axis_size("row")
    col_count = lax.axis_size("col")
    gvecs = g_rows * row_count * col_count
    row_width = row_tiles * tile_size
    col_width = col_tiles * tile_size
    lifted = (
        psi.reshape(1, g_rows, row_tiles, row_count, tile_size),
        hpsi.reshape(1, g_rows, row_tiles, row_count, tile_size),
    )
    swapped = in_one_piece((lifted[0], lifted[1]), "row", 3, 0, 1)
    joined = in_one_piece_2((swapped[0], swapped[1]), "col", 1, 0)
    psi_rows = joined[0].reshape(gvecs, row_width)
    hpsi_rows = joined[1].reshape(gvecs, row_width)
    lowered = (
        psi.reshape(g_rows, col_tiles, col_count, tile_size),
        hpsi.reshape(g_rows, col_tiles, col_count, tile_size),
    )
    moved = in_one_piece((lowered[0], lowered[1]), "col", 2, 0, 1)
    stacked = in_one_piece_2((moved[0], moved[1]), "row", 0, 1)
    psi_cols = stacked[0].reshape(gvecs, col_width)
    hpsi_cols = stacked[1].reshape(gvecs, col_width)
    reduced = 0.5 * (inner(psi_rows, hpsi_cols) + inner(hpsi_rows, psi_cols))
    correlation = inner(psi_rows, psi_cols) / float(gvecs)
    a_rows = lax.all_gather(reduced, "col")
    updated, diagonal, offdiag = reduce_panel(a_rows, row_count)
    flat = eigvec.reshape(row_width, col_width)
    rotated = lax.psum_scatter(
        jnp.dot(psi_rows, flat, preferred_element_type=jnp.float32),
        "row",
        scatter_dimension=0,
        tiled=True,
    )
    tile_shape = (row_tiles, 1, tile_size, col_tiles, 1, tile_size)
    return (
        correlation.reshape(tile_shape),
        updated.reshape(tile_shape),
        diagonal[0, :PB],
        offdiag[0, :PB],
        rotated.astype(jnp.bfloat16).reshape(rotated.shape[0], col_tiles, 1, tile_size),
    )


def solution(mesh):
    return jax.shard_map(
        on_device,
        mesh=mesh,
        in_specs=(
            P(("row", "col"), None),
            P(("row", "col"), None),
            P(None, "row", None, None, "col", None),
        ),
        out_specs=(
            P(None, "row", None, None, "col", None),
            P(None, "row", None, None, "col", None),
            P(),
            P(),
            P("row", None, "col", None),
        ),
        check_vma=False,
    )
```

time: 924 us -> 360 us (0.39)
  matrix products: 205 us -> 13.8 us
  starting transfers between devices: 185 us -> 0.34 us
  other arithmetic: 131 us -> 1.22 us
  Pallas kernels: 0 us -> 92.7 us
  loops' own time: 68.4 us -> 0 us
  local copies, waits for them, and re-layouts: 85.7 us -> 54 us
  blocking collectives: 61.3 us -> 32.6 us
  waiting for transfers between devices: 169 us -> 151 us
    all_to_all x33 -> x0, starting transfers between devices: 185 us -> none  [copy_for_each(): lax.all_to_all(jnp.broadcast_to(array[None], (length, *array.shape)), axi...]
    dot_general x98 -> x0, matrix products: 180 us -> none  [the longest x16 45.5 us: reflect(): jnp.dot(vector, images, precision=highest)]
    pallas_call x0 -> x1, Pallas kernels: none -> 92.7 us  [reduce_panel(): pl.pallas_call(panel_kernel, out_shape=(jax.ShapeDtypeStruct((height * wi...]
    all_to_all x33 -> x0, waiting for transfers between devices: 84.9 us -> none  [copy_for_each(): lax.all_to_all(jnp.broadcast_to(array[None], (length, *array.shape)), axi...]
    select_n x64 -> x0, other arithmetic: 72.1 us -> none  [the longest x16 61 us: reflect(): images = jnp.where(pick[None, :], image[:, None], images)]
    another operation x1 -> x0, loops' own time: 68.4 us -> none  [on_device(): vecs, images, diagonal, offdiag = lax.fori_loop(0, PB, reflect, start_state)]
    all_gather x0 -> x1, waiting for transfers between devices: none -> 61.6 us  [on_device(): a_rows = lax.all_gather(reduced, 'col')]
    while x16 -> x0, other arithmetic: 37.7 us -> none
  transfers between devices with their start and end apart: 36 -> 4, of which waited for: 19 -> 3; matrix products, arithmetic and copies ran while one was open for 45% -> 8% of each run, Pallas kernels for 0% -> 26%
where the time goes in v1:
time: 360 us; the launch traced here: 359 us
  waiting for transfers between devices  151 us (42%)
  Pallas kernels  92.7 us (26%)
  local copies, waits for them, and re-layouts  54 us (15%)
  blocking collectives  32.6 us (9%)
  between operations  13.9 us (4%)
  matrix products  13.8 us (4%)
    pallas_call x1, Pallas kernels, reduce_panel(): pl.pallas_call(panel_kernel, out_shape=(jax.ShapeDtypeStruct((height * wi...  92.7 us
    all_gather x2, waiting for transfers between devices, in_one_piece_2(): lax.all_gather(both, axis, axis=dim, tiled=True)  89 us
    all_gather x1, waiting for transfers between devices, on_device(): a_rows = lax.all_gather(reduced, 'col')  61.6 us
    all_to_all x2, blocking collectives, in_one_piece(): lax.all_to_all(both, axis, split_axis=split_dim, concat_axis=concat_dim,...  32.6 us
    unnamed x15, local copies, waits for them, and re-layouts  25.4 us
    slice x4, local copies, waits for them, and re-layouts, in_one_piece_2(): lax.slice_in_dim(whole, at, at + a.shape[along], axis=along)  24.9 us
    dot_general x3, matrix products, inner(): lax.dot_general(left, right, (((0,), (0,)), ((), ())), preferred_element_...  9.17 us
  transfers between devices with their start and end apart: 4, of which 3 were waited for; matrix products, arithmetic and copies ran while one was open for 8% of the time, Pallas kernels for 26%

profile of v1, /device:TPU:1, one launch (start us, length us, event | category | flops | bytes accessed | tf_op | source)
XLA Modules:
  0.0 359.2 jit_solution(6673136903246456536)
XLA Ops:
  7.2 1.0 copy.64
  8.2 1.0 copy.65
  9.3 0.2 copy.51
  9.5 17.2 %all_to_all.36 = bf16[1,64,2,16,128]{4,1,2,0,3:T(8,128)(2,1)S(1)} all-to-all(bf16[1,64,2,16,128]{4,1,2,0,3:T(8,128)(2,1)S(1)} %copy.51), channel_id=1, replica_groups=mesh['row'=16,'col'=8] {'row'}, dimensions={3} | all-to-all | bytes 1048576 | tf_op jit(solution)/shard_map/all_to_all | solution.py:15
  26.8 1.1 copy.52
  28.0 0.1 pad_maximum_fusion.2
  28.1 0.1 copy.54
  28.1 15.4 %all_to_all.37 = bf16[32,8,8,128]{3,1,0,2:T(8,128)(2,1)} all-to-all(bf16[32,8,8,128]{3,1,0,2:T(8,128)(2,1)S(1)} %copy.54), channel_id=1, replica_groups=mesh['row'=16,'col'=8] {'col'}, dimensions={2} | all-to-all | bytes 1048576 | tf_op jit(solution)/shard_map/all_to_all | solution.py:15
  43.6 54.7 %all-gather.5.cloned.1.call-done = bf16[32,256,2,1,128]{4,0,3,2,1:T(8,128)(2,1)} async-done(((bf16[32,32,2,1,128]{4,0,3,2,1:T(8,128)(2,1)}), bf16[32,256,2,1,128]{4,0,3,2,1:T(8,128)(2,1)}) %all-gather.5.cloned.1.call-update) | async-done | bytes 4194320 | tf_op jit(solution)/shard_map/all_gather | solution.py:27
  98.3 4.9 %fusion.5 = (bf16[16,256,2,1,128]{4,0,3,2,1:T(8,128)(2,1)}, bf16[16,256,2,1,128]{4,0,3,2,1:T(8,128)(2,1)}) fusion(bf16[32,256,2,1,128]{4,0,3,2,1:T(8,128)(2,1)} %all-gather.5.cloned.1.call-done), kind=kLoop, calls=%fused_computation.12 | loop fusion | bytes 8388608 | tf_op jit(solution)/shard_map/slice | solution.py:29
  103.2 3.8 %copy.58 = bf16[16,256,2,1,128]{1,0,4,2,3:T(8,128)(2,1)S(1)} copy(bf16[16,256,2,1,128]{4,0,3,2,1:T(8,128)(2,1)} %get-tuple-element.43) | data formatting | bytes 4194304 | tf_op jit(solution)/shard_map/slice | solution.py:29
  107.0 2.3 copy.69
  109.3 4.9 %copy.53 = bf16[16,256,2,1,128]{1,0,4,2,3:T(8,128)(2,1)} copy(bf16[16,256,2,1,128]{4,0,3,2,1:T(8,128)(2,1)} %get-tuple-element.44) | data formatting | bytes 4194304 | tf_op jit(solution)/shard_map/slice | solution.py:29
  114.2 2.6 copy.66
  116.8 34.3 %all-gather.7.cloned.1.call-done = bf16[4096,8,1,128]{3,1,2,0:T(8,128)(2,1)} async-done(((bf16[256,8,1,128]{3,1,2,0:T(8,128)(2,1)}), bf16[4096,8,1,128]{3,1,2,0:T(8,128)(2,1)}) %all-gather.7.cloned.1.call-update) | async-done | bytes 8388624 | tf_op jit(solution)/shard_map/all_gather | solution.py:27
  151.1 11.3 %fusion.4 = (bf16[4096,4,1,128]{3,1,2,0:T(4,128)(2,1)}, bf16[4096,4,1,128]{3,1,2,0:T(4,128)(2,1)}) fusion(bf16[4096,8,1,128]{3,1,2,0:T(8,128)(2,1)} %all-gather.7.cloned.1.call-done), kind=kLoop, calls=%fused_computation.11 | loop fusion | bytes 16777216 | tf_op jit(solution)/shard_map/slice | solution.py:29
  162.4 7.5 %copy.63 = bf16[4096,4,1,128]{0,3,1,2:T(8,128)(2,1)} copy(bf16[4096,4,1,128]{3,1,2,0:T(4,128)(2,1)} %get-tuple-element.41) | data formatting | bytes 8388608
  169.9 7.5 %copy.62 = bf16[4096,4,1,128]{0,3,1,2:T(8,128)(2,1)} copy(bf16[4096,4,1,128]{3,1,2,0:T(4,128)(2,1)} %get-tuple-element.42) | data formatting | bytes 8388608
  177.5 3.6 %fusion.7 = f32[256,512]{1,0:T(8,128)S(1)} fusion(bf16[4096,256]{0,1:T(8,128)(2,1)S(1)} %bitcast.61, bf16[4096,512]{0,1:T(8,128)(2,1)} %bitcast.68), kind=kOutput, calls=%fused_computation.14 | convolution fusion | flops 1073741824 | bytes 6815744 | tf_op jit(solution)/shard_map/dot_general | solution.py:35
  181.1 0.5 copy-done.2
  181.6 2.1 fusion
  183.7 0.2 reduce-scatter.2.cloned.1.call-start
  183.9 4.6 %fusion.1 = f32[4096,512]{1,0:T(8,128)} fusion(bf16[4096,256]{0,1:T(8,128)(2,1)S(1)} %bitcast.62, bf16[32,8,4,128]{3,2,1,0:T(4,128)(2,1)S(1)} %bitcast.77), kind=kOutput, calls=%fused_computation.6 | convolution fusion | flops 1073741824 | bytes 10747904 | tf_op jit(solution)/shard_map/dot_general | solution.py:280
  188.6 3.5 convolution_multiply_fusion
  192.1 1.0 reshape.52
  193.0 61.6 %all-gather.9.cloned.1.call-done = f32[2048,512]{1,0:T(8,128)} async-done(((f32[256,512]{1,0:T(8,128)}), f32[2048,512]{1,0:T(8,128)}) %all-gather.9.cloned.1.call-update) | async-done | bytes 4194320 | tf_op jit(solution)/shard_map/all_gather | solution.py:276
  254.7 2.2 copy-done
  256.9 92.7 %panel.1 = (f32[1024,128]{1,0:T(8,128)S(1)}, f32[8,128]{1,0:T(8,128)S(1)}, f32[8,128]{1,0:T(8,128)S(1)}) custom-call(f32[8,256,512]{2,1,0:T(8,128)S(1)} %bitcast.59), custom_call_target="tpu_custom_call" | custom-call | tf_op jit(solution)/shard_map/panel/pallas_call | solution.py:217
  349.6 0.5 slice_bitcast_fusion
  350.1 1.1 convert_element_type.3
  351.2 0.8 reshape.57
  351.9 0.8 copy.76
  (17 shorter events, 0.3 us)
Async XLA Ops:
  7.2 91.1 %all-gather.5.cloned.1.call-start = ((), (), s32[]{:S(2)}) async-start(), calls=%async_computation.3 | async-start | bytes 4718592 | tf_op jit(solution)/shard_map/all_gather | solution.py:27
  28.0 123.2 %all-gather.7.cloned.1.call-start = ((), (), s32[]{:S(2)}) async-start(), calls=%async_computation.4 | async-start | bytes 8912896 | tf_op jit(solution)/shard_map/all_gather | solution.py:27
  43.6 211.1 %all-gather.9.cloned.1.call-start = ((), (), s32[]{:S(2)}) async-start(), calls=%async_computation.6 | async-start | bytes 4718592 | tf_op jit(solution)/shard_map/all_gather | solution.py:276
  177.5 3.6 %copy-start.1 = (bf16[4096,4,1,128]{0,3,1,2:T(8,128)(2,1)S(1)}, bf16[4096,4,1,128]{0,3,1,2:T(8,128)(2,1)}, u32[]{:S(2)}) copy-start(bf16[4096,4,1,128]{0,3,1,2:T(8,128)(2,1)} %copy.62) | copy-start | bytes 12582916
  177.5 4.1 %copy-start.2 = (bf16[32,8,16,256]{3,1,2,0:T(8,128)(2,1)S(1)}, bf16[32,8,16,256]{3,1,2,0:T(8,128)(2,1)}, u32[]{:S(2)}) copy-start(bf16[32,8,16,256]{3,1,2,0:T(8,128)(2,1)} %copy.69) | copy-start | bytes 6291460
  181.6 2.3 copy-start.3
  183.7 166.4 %reduce-scatter.2.cloned.1.call-start = ((), (), s32[]{:S(2)}) async-start(), calls=%async_computation.5 | async-start | bytes 8912896 | tf_op jit(solution)/shard_map/reduce_scatter | solution.py:279
  254.7 2.2 copy-start
Sparse Core Ops, SparseCore 0:
  28.1 70.1 all-gather.4
  100.0 51.1 all-gather.6
  183.8 70.8 all-gather.8
  256.9 72.0 reduce-scatter.1

commit v2 on v1

--- a/solution.py
+++ b/solution.py
@@ -7,34 +7,6 @@
 
 PB = 16
 MESH = pl.DeviceIdType.MESH
-
-
-def in_one_piece(arrays, axis, split_dim, concat_dim, along):
-    both = jnp.concatenate(arrays, axis=along)
-    whole, at, gathered = (
-        lax.all_to_all(both, axis, split_axis=split_dim, concat_axis=concat_dim, tiled=True),
-        0,
-        [],
-    )
-    for a in arrays:
-        gathered.append(lax.slice_in_dim(whole, at, at + a.shape[along], axis=along))
-        at += a.shape[along]
-    return tuple(gathered)
-
-
-def in_one_piece_2(arrays, axis, dim, along):
-    both = jnp.concatenate(arrays, axis=along)
-    whole, at, gathered = (lax.all_gather(both, axis, axis=dim, tiled=True), 0, [])
-    for a in arrays:
-        gathered.append(lax.slice_in_dim(whole, at, at + a.shape[along], axis=along))
-        at += a.shape[along]
-    return tuple(gathered)
-
-
-def inner(left, right):
-    return lax.dot_general(
-        left, right, (((0,), (0,)), ((), ())), preferred_element_type=jnp.float32
-    )
 
 
 def split_three(x):
@@ -245,42 +217,241 @@
     )(a_rows)
 
 
+def lattice(row, col):
+    pair = {"row": lax.div(row, 8), "col": lax.div(col, 4)}
+    ring = {"row": lax.rem(lax.div(row, 2), 4), "col": lax.rem(col, 4)}
+    return pair, ring
+
+
+def front_kernel(
+    psi_ref,
+    hpsi_ref,
+    a_ref,
+    corr_ref,
+    by_row,
+    by_col,
+    total_a,
+    total_s,
+    send_sem,
+    swap_sem,
+    ring_sem,
+    core_sem,
+):
+    rows = lax.axis_size("row")
+    cols = lax.axis_size("col")
+    row = lax.axis_index("row")
+    col = lax.axis_index("col")
+    tile = 128
+    halves = by_row.shape[4] // tile
+    blocks = by_col.shape[4] // tile
+    pair, ring = lattice(row, col)
+    core = lax.rem(row, 2)
+    inputs = (psi_ref, hpsi_ref)
+
+    def place(axis, across, along):
+        p = lax.rem(pair[axis] + across, 2)
+        q = lax.rem(ring[axis] + along + 4, 4)
+        return p * 8 + q * 2 + core if axis == "row" else p * 4 + q
+
+    row_order = sorted(range(1, rows), key=lambda d: -min(d, rows - d))
+    row_peers = [lax.rem(row + d, rows) for d in row_order]
+    col_peers = [lax.rem(col + d, cols) for d in range(1, cols)]
+    barrier = pltpu.get_barrier_semaphore()
+    for r in row_peers:
+        pl.semaphore_signal(
+            barrier, inc=1, device_id={"row": r, "col": col}, device_id_type=MESH
+        )
+    for c in col_peers:
+        pl.semaphore_signal(
+            barrier, inc=1, device_id={"row": row, "col": c}, device_id_type=MESH
+        )
+    pl.semaphore_wait(barrier, rows + cols - 2)
+
+    def send(source, target, sem, where):
+        pltpu.make_async_remote_copy(
+            src_ref=source,
+            dst_ref=target,
+            send_sem=send_sem,
+            recv_sem=sem,
+            device_id={"row": row, "col": col, **where},
+            device_id_type=MESH,
+        ).start()
+
+    def lanes(tile_index):
+        return pl.ds(pl.multiple_of(tile_index * tile, tile), tile)
+
+    for n, source in enumerate(inputs):
+        for r in row_peers:
+            for h in range(halves):
+                send(
+                    source.at[:, lanes(h * rows + r)],
+                    by_row.at[n, col, row, :, h * tile : (h + 1) * tile],
+                    swap_sem.at[n, 0],
+                    {"row": r},
+                )
+        for c in col_peers:
+            for b in range(blocks):
+                send(
+                    source.at[:, lanes(b * cols + c)],
+                    by_col.at[n, row, col, :, b * tile : (b + 1) * tile],
+                    swap_sem.at[n, 1],
+                    {"col": c},
+                )
+    for n, source in enumerate(inputs):
+        for h in range(halves):
+            by_row[n, col, row, :, h * tile : (h + 1) * tile] = source[:, lanes(h * rows + row)]
+        for b in range(blocks):
+            by_col[n, row, col, :, b * tile : (b + 1) * tile] = source[:, lanes(b * cols + col)]
+
+    def arrived(ref, sem):
+        pltpu.make_async_copy(ref, ref, sem).wait()
+
+    kinds = [(n, part) for n in range(2) for part in range(2)]
+    axes = ("col", "row")
+    held = (by_row, by_col)
+
+    def piece(n, part, across, along, half=None):
+        whole = held[part].at[n, place(axes[part], across, along)]
+        if half is None:
+            return whole
+        size = whole.shape[0] // 2
+        return whole.at[pl.ds(half * size, size)]
+
+    def along_ring(n, part, across, along, way, half, sem):
+        what = piece(n, part, across, along, half)
+        where = {axes[part]: place(axes[part], 0, way)}
+        send(what, what, ring_sem.at[n, part, sem], where)
+
+    def to_core(n, part, across, along, half=None):
+        if part == 1:
+            what = piece(n, part, across, along, half)
+            send(what, what, core_sem.at[n], {"row": row + 1 - 2 * core})
+
+    def wait_ring(n, part, across, along, half, sem):
+        arrived(piece(n, part, across, along, half), ring_sem.at[n, part, sem])
+
+    for n, part in kinds:
+        count = (rows if part == 0 else cols) - 1
+        mine = (col if part == 0 else row,)
+        arrived(held[part].at[n, mine[0], pl.ds(0, count)], swap_sem.at[n, part])
+        along_ring(n, part, 0, 0, 1, None, 0)
+        along_ring(n, part, 0, 0, -1, None, 1)
+        what = piece(n, part, 0, 0)
+        send(what, what, ring_sem.at[n, part, 2], {axes[part]: place(axes[part], 1, 0)})
+        to_core(n, part, 0, 0)
+    for n, part in kinds:
+        wait_ring(n, part, 0, -1, None, 0)
+        along_ring(n, part, 0, -1, 1, 0, 3)
+        to_core(n, part, 0, -1)
+        wait_ring(n, part, 0, 1, None, 1)
+        along_ring(n, part, 0, 1, -1, 1, 4)
+        to_core(n, part, 0, 1)
+        wait_ring(n, part, 1, 0, None, 2)
+        along_ring(n, part, 1, 0, 1, None, 5)
+        along_ring(n, part, 1, 0, -1, None, 6)
+        to_core(n, part, 1, 0)
+    for n, part in kinds:
+        wait_ring(n, part, 0, 2, 0, 3)
+        to_core(n, part, 0, 2, 0)
+        wait_ring(n, part, 0, 2, 1, 4)
+        to_core(n, part, 0, 2, 1)
+        wait_ring(n, part, 1, -1, None, 5)
+        along_ring(n, part, 1, -1, 1, 0, 7)
+        to_core(n, part, 1, -1)
+        wait_ring(n, part, 1, 1, None, 6)
+        along_ring(n, part, 1, 1, -1, 1, 8)
+        to_core(n, part, 1, 1)
+    for n, part in kinds:
+        wait_ring(n, part, 1, 2, 0, 7)
+        to_core(n, part, 1, 2, 0)
+        wait_ring(n, part, 1, 2, 1, 8)
+        to_core(n, part, 1, 2, 1)
+    for n in range(2):
+        arrived(by_col.at[n, pl.ds(0, rows // 2)], core_sem.at[n])
+
+    total_a[...] = jnp.zeros_like(total_a)
+    total_s[...] = jnp.zeros_like(total_s)
+
+    def product(left, right):
+        return lax.dot_general(
+            left, right, (((0,), (0,)), ((), ())), preferred_element_type=jnp.float32
+        )
+
+    def add(c, carry):
+        depth = rows * by_row.shape[3]
+        psi_r = by_row[0, c].reshape(depth, halves * tile)
+        hpsi_r = by_row[1, c].reshape(depth, halves * tile)
+        psi_c = by_col[0, :, c].reshape(depth, blocks * tile)
+        hpsi_c = by_col[1, :, c].reshape(depth, blocks * tile)
+        total_a[...] += product(psi_r, hpsi_c) + product(hpsi_r, psi_c)
+        total_s[...] += product(psi_r, psi_c)
+        return carry
+
+    lax.fori_loop(0, cols, add, 0)
+    gvecs = rows * cols * by_row.shape[3]
+    a_ref[...] = 0.5 * total_a[...]
+    for b in range(blocks):
+        corr_ref[pl.ds(b, halves * tile, stride=blocks), :] = total_s[
+            :, b * tile : (b + 1) * tile
+        ] * (1.0 / gvecs)
+
+    def sent(ref):
+        pltpu.make_async_copy(ref, ref, send_sem).wait()
+
+    for n in range(2):
+        sent(by_row.at[n, 0, pl.ds(0, rows - 1)])
+        sent(by_col.at[n, 0, pl.ds(0, cols - 1)])
+        for part in range(2):
+            for _ in range(5):
+                sent(held[part].at[n, 0])
+            for _ in range(2):
+                sent(held[part].at[n, 0])
+        sent(by_col.at[n, pl.ds(0, rows // 2)])
+
+
+def reduce_front(psi, hpsi, rows, cols, halves, blocks):
+    tile = 128
+    vmem = pl.BlockSpec(memory_space=pltpu.VMEM)
+    height, width = halves * tile, blocks * tile
+    return pl.pallas_call(
+        front_kernel,
+        out_shape=(
+            jax.ShapeDtypeStruct((height, width), jnp.float32),
+            jax.ShapeDtypeStruct((height * blocks, tile), jnp.float32),
+        ),
+        in_specs=[vmem, vmem],
+        out_specs=(vmem, vmem),
+        scratch_shapes=[
+            pltpu.VMEM((2, cols, rows, psi.shape[0], height), psi.dtype),
+            pltpu.VMEM((2, rows, cols, psi.shape[0], width), psi.dtype),
+            pltpu.VMEM((height, width), jnp.float32),
+            pltpu.VMEM((height, width), jnp.float32),
+            pltpu.SemaphoreType.DMA,
+            pltpu.SemaphoreType.DMA((2, 2)),
+            pltpu.SemaphoreType.DMA((2, 2, 9)),
+            pltpu.SemaphoreType.DMA((2,)),
+        ],
+        compiler_params=pltpu.CompilerParams(
+            collective_id=1, has_side_effects=True, vmem_limit_bytes=48 * 1024 * 1024
+        ),
+        name="front",
+    )(psi, hpsi)
+
+
 def on_device(psi, hpsi, eigvec):
-    g_rows = psi.shape[0]
-    row_tiles = eigvec.shape[0]
-    tile_size = eigvec.shape[2]
-    col_tiles = eigvec.shape[3]
+    row_tiles, _, tile_size, col_tiles = eigvec.shape[:4]
     row_count = lax.axis_size("row")
     col_count = lax.axis_size("col")
-    gvecs = g_rows * row_count * col_count
-    row_width = row_tiles * tile_size
-    col_width = col_tiles * tile_size
-    lifted = (
-        psi.reshape(1, g_rows, row_tiles, row_count, tile_size),
-        hpsi.reshape(1, g_rows, row_tiles, row_count, tile_size),
-    )
-    swapped = in_one_piece((lifted[0], lifted[1]), "row", 3, 0, 1)
-    joined = in_one_piece_2((swapped[0], swapped[1]), "col", 1, 0)
-    psi_rows = joined[0].reshape(gvecs, row_width)
-    hpsi_rows = joined[1].reshape(gvecs, row_width)
-    lowered = (
-        psi.reshape(g_rows, col_tiles, col_count, tile_size),
-        hpsi.reshape(g_rows, col_tiles, col_count, tile_size),
-    )
-    moved = in_one_piece((lowered[0], lowered[1]), "col", 2, 0, 1)
-    stacked = in_one_piece_2((moved[0], moved[1]), "row", 0, 1)
-    psi_cols = stacked[0].reshape(gvecs, col_width)
-    hpsi_cols = stacked[1].reshape(gvecs, col_width)
-    reduced = 0.5 * (inner(psi_rows, hpsi_cols) + inner(hpsi_rows, psi_cols))
-    correlation = inner(psi_rows, psi_cols) / float(gvecs)
+    reduced, correlation = reduce_front(psi, hpsi, row_count, col_count, row_tiles, col_tiles)
+    reduced, psi, eigvec = lax.optimization_barrier((reduced, psi, eigvec))
     a_rows = lax.all_gather(reduced, "col")
+    psi_rows = lax.all_gather(psi, "col", axis=0, tiled=True)
+    rotation = lax.all_gather(eigvec, "row", axis=1, tiled=True)
     updated, diagonal, offdiag = reduce_panel(a_rows, row_count)
-    flat = eigvec.reshape(row_width, col_width)
-    rotated = lax.psum_scatter(
-        jnp.dot(psi_rows, flat, preferred_element_type=jnp.float32),
-        "row",
-        scatter_dimension=0,
-        tiled=True,
+    rotated = jnp.dot(
+        psi_rows,
+        rotation.reshape(psi.shape[1], col_tiles * tile_size),
+        preferred_element_type=jnp.float32,
     )
     tile_shape = (row_tiles, 1, tile_size, col_tiles, 1, tile_size)
     return (

time: 360 us -> 249 us (0.69)
  waiting for transfers between devices: 151 us -> 67.5 us
  Pallas kernels: 92.7 us -> 156 us
  local copies, waits for them, and re-layouts: 54 us -> 6.95 us
  blocking collectives: 32.6 us -> 0 us
  matrix products: 13.8 us -> 4.07 us
    all_gather x2, waiting for transfers between devices: 89 us -> 0.01 us  [the longest x1 0.01 us: on_device(): psi_rows = lax.all_gather(psi, 'col', axis=0, tiled=True)]
    pallas_call x0 -> x1, Pallas kernels: none -> 64.2 us  [reduce_front(): pl.pallas_call(front_kernel, out_shape=(jax.ShapeDtypeStruct((height, wid...]
    all_to_all x2 -> x0, blocking collectives: 32.6 us -> none  [in_one_piece(): lax.all_to_all(both, axis, split_axis=split_dim, concat_axis=concat_dim,...]
    slice x5 -> x0, local copies, waits for them, and re-layouts: 25 us -> none  [the longest x4 24.9 us: in_one_piece_2(): lax.slice_in_dim(whole, at, at + a.shape[along], axis=along)]
    unnamed x15 -> x8, local copies, waits for them, and re-layouts: 25.4 us -> 5.67 us
    dot_general x4 -> x1, matrix products: 13.8 us -> 4.07 us  [on_device(): jnp.dot(psi_rows, rotation.reshape(psi.shape[1], col_tiles * tile_size),...]
    all_gather x1, waiting for transfers between devices: 61.6 us -> 66.1 us  [on_device(): a_rows = lax.all_gather(reduced, 'col')]
  transfers between devices with their start and end apart: 4 -> 3, of which waited for: 3 -> 1; matrix products, arithmetic and copies ran while one was open for 8% -> 0% of each run, Pallas kernels for 26% -> 37%
where the time goes in v2:
time: 249 us
  Pallas kernels  156 us (63%)
  waiting for transfers between devices  67.5 us (27%)
  between operations  13.8 us (6%)
  local copies, waits for them, and re-layouts  6.95 us (3%)
  matrix products  4.07 us (2%)
    pallas_call x1, Pallas kernels, reduce_panel(): pl.pallas_call(panel_kernel, out_shape=(jax.ShapeDtypeStruct((height * wi...  92.2 us
    all_gather x1, waiting for transfers between devices, on_device(): a_rows = lax.all_gather(reduced, 'col')  66.1 us
    pallas_call x1, Pallas kernels, reduce_front(): pl.pallas_call(front_kernel, out_shape=(jax.ShapeDtypeStruct((height, wid...  64.2 us
    unnamed x8, local copies, waits for them, and re-layouts  5.67 us
  transfers between devices with their start and end apart: 3, of which 1 were waited for; matrix products, arithmetic and copies ran while one was open for 0% of the time, Pallas kernels for 37%

profile of v2, /device:TPU:1, one launch (start us, length us, event | category | flops | bytes accessed | tf_op | source)
XLA Modules:
  0.0 248.8 jit_solution(16940386498776809706)
XLA Ops:
  7.2 0.0 all-gather.9.cloned.1.call-start
  7.2 0.0 copy-start.1
  7.2 0.9 copy-done.1
  8.2 0.0 copy-start.2
  8.2 0.9 copy-done.2
  9.1 64.2 %front.1 = (f32[256,512]{1,0:T(8,128)}, f32[1024,128]{1,0:T(8,128)S(1)}) custom-call(bf16[32,4096]{1,0:T(8,128)(2,1)S(1)} %copy-done.1, bf16[32,4096]{1,0:T(8,128)(2,1)S(1)} %copy-done.2), custom_call_target="tpu_custom_call" | custom-call | tf_op jit(solution)/shard_map/front/pallas_call | solution.py:416
  73.3 0.0 all-gather.9.cloned.1.call-update
  73.3 0.0 all-gather.5.cloned.1.call-start
  73.4 0.7 all-gather.5.cloned.1.call-update
  74.1 0.0 all-gather.7.cloned.1.call-start
  74.1 0.7 all-gather.7.cloned.1.call-update
  74.8 66.1 %all-gather.9.cloned.1.call-done = f32[2048,512]{1,0:T(8,128)} async-done(((f32[256,512]{1,0:T(8,128)}), f32[2048,512]{1,0:T(8,128)}) %all-gather.9.cloned.1.call-update) | async-done | bytes 4194320 | tf_op jit(solution)/shard_map/all_gather | solution.py:447
  140.9 0.0 copy-start
  140.9 2.2 copy-done
  143.1 92.2 %panel.1 = (f32[1024,128]{1,0:T(8,128)S(1)}, f32[8,128]{1,0:T(8,128)S(1)}, f32[8,128]{1,0:T(8,128)S(1)}) custom-call(f32[8,256,512]{2,1,0:T(8,128)S(1)} %bitcast.21), custom_call_target="tpu_custom_call" | custom-call | tf_op jit(solution)/shard_map/panel/pallas_call | solution.py:189
  235.3 0.5 slice_bitcast_fusion
  235.8 0.0 all-gather.5.cloned.1.call-done
  235.8 0.0 all-gather.7.cloned.1.call-done
  235.8 4.1 %fusion.3 = bf16[256,512]{1,0:T(8,128)(2,1)S(1)} fusion(bf16[256,4096]{1,0:T(8,128)(2,1)} %all-gather.5.cloned.1.call-done, bf16[512,8,4,128]{3,2,1,0:T(4,128)(2,1)} %bitcast.25), kind=kOutput, calls=%fused_computation.3 | convolution fusion | flops 1073872896 | bytes 6553600 | tf_op jit(solution)/shard_map/dot_general | solution.py:451
  239.9 0.8 reshape.25
  240.7 0.8 copy.20
  241.5 0.8 copy.21
Async XLA Ops:
  7.2 133.7 %all-gather.9.cloned.1.call-start = ((), (), s32[]{:S(2)}) async-start(), calls=%async_computation.2 | async-start | bytes 4718592 | tf_op jit(solution)/shard_map/all_gather | solution.py:447
  7.2 1.0 copy-start.1
  8.2 0.9 copy-start.2
  73.3 162.5 %all-gather.5.cloned.1.call-start = ((), (), s32[]{:S(2)}) async-start(), calls=%async_computation | async-start | bytes 2359296 | tf_op jit(solution)/shard_map/all_gather | solution.py:448
  74.1 161.8 %all-gather.7.cloned.1.call-start = ((), (), s32[]{:S(2)}) async-start(), calls=%async_computation.1 | async-start | bytes 4456448 | tf_op jit(solution)/shard_map/all_gather | solution.py:449
  140.9 2.2 copy-start
Sparse Core Ops, SparseCore 0:
  73.4 67.4 all-gather.8
  143.2 51.7 all-gather.4
  196.7 36.6 all-gather.6

commit v3 on v2

--- a/solution.py
+++ b/solution.py
@@ -19,10 +19,17 @@
 
 def panel_kernel(
     a_ref,
+    psi_ref,
+    eig_ref,
     updated_ref,
     diag_ref,
     off_ref,
-    panel_out,
+    rotated_ref,
+    psi_rows,
+    eig_cols,
+    rotated,
+    rotated_tiles,
+    a_plane,
     panel_in,
     panel,
     vecs,
@@ -33,51 +40,217 @@
     parts_in,
     whole,
     send_sem,
+    ring_sem,
     panel_sem,
     parts_sem,
+    eig_sem,
+    core_sem,
+    psi_sem,
 ):
     rows = lax.axis_size("row")
     cols = lax.axis_size("col")
     row = lax.axis_index("row")
     col = lax.axis_index("col")
-    height = a_ref.shape[1]
+    height = a_ref.shape[0]
     tile = 128
-    blocks = a_ref.shape[2] // tile
+    blocks = a_ref.shape[1] // tile
     halves = height // tile
     tiles = rows * halves
-    order = sorted(range(1, rows), key=lambda d: -min(d, rows - d))
-    peers = [{"row": lax.rem(row + d, rows), "col": col} for d in order]
+    turns = cols // 2
+    pair = lax.div(col, turns)
+    ring = lax.rem(col, turns)
+    order = sorted(
+        ((d, e) for d in range(rows) for e in range(2) if d + e > 0),
+        key=lambda de: -min(de[0], rows - de[0]) - 4 * de[1],
+    )
+    peers = [
+        {"row": lax.rem(row + d, rows), "col": lax.rem(pair + e, 2) * turns + ring}
+        for d, e in order
+    ]
+    around = [{"row": row, "col": pair * turns + lax.rem(ring + d, turns)} for d in (1, 3, 2)]
     barrier = pltpu.get_barrier_semaphore()
-    for peer in peers:
+    for peer in peers + around:
         pl.semaphore_signal(barrier, inc=1, device_id=peer, device_id_type=MESH)
-    pl.semaphore_wait(barrier, rows - 1)
+    pl.semaphore_wait(barrier, len(peers) + len(around))
+
+    def send(source, target, recv, peer):
+        pltpu.make_async_remote_copy(
+            src_ref=source,
+            dst_ref=target,
+            send_sem=send_sem,
+            recv_sem=recv,
+            device_id=peer,
+            device_id_type=MESH,
+        ).start()
 
     def to_peers(source, target, recv):
         for peer in peers:
-            pltpu.make_async_remote_copy(
-                src_ref=source,
-                dst_ref=target,
-                send_sem=send_sem,
-                recv_sem=recv,
-                device_id=peer,
-                device_id_type=MESH,
-            ).start()
-
-    for half in range(halves):
-        first = a_ref[0, half * tile : (half + 1) * tile, 0:tile]
-        panel_out[:, half, :] = jnp.transpose(first)[0:PB, :]
-    to_peers(panel_out, panel_in.at[row], panel_sem)
-    panel_in[row] = panel_out[...]
+            send(source, target, recv, peer)
+
+    def arrived(ref, sem):
+        pltpu.make_async_copy(ref, ref, sem).wait()
+
+    @pl.when(col == 0)
+    def _():
+        for half in range(halves):
+            first = a_ref[half * tile : (half + 1) * tile, 0:tile]
+            panel_in[row, :, half, :] = jnp.transpose(first)[0:PB, :]
+        for peer in around:
+            send(panel_in.at[row], panel_in.at[row], panel_sem.at[0], peer)
+
+    above, below = lax.rem(ring + 1, turns), lax.rem(ring + turns - 1, turns)
+    send(a_ref, a_plane.at[ring], ring_sem.at[0], around[0])
+    send(a_ref, a_plane.at[ring], ring_sem.at[1], around[1])
+
+    row_pair, row_ring, core = lax.div(row, 8), lax.rem(lax.div(row, 2), 4), lax.rem(row, 2)
+
+    def eig_place(across, along):
+        p = lax.rem(row_pair + across, 2)
+        return p * 8 + lax.rem(row_ring + along + 4, 4) * 2 + core
+
+    def psi_place(across, along):
+        return lax.rem(pair + across, 2) * turns + lax.rem(ring + along + turns, turns)
+
+    def piece(held, index, half):
+        whole = held.at[index]
+        if half is None:
+            return whole
+        size = whole.shape[0] // 2
+        return whole.at[pl.ds(half * size, size)]
+
+    def eig_send(across, along, way, half, sem):
+        what = piece(eig_cols, eig_place(across, along), half)
+        to = eig_place(1, 0) if way is None else eig_place(0, way)
+        send(what, what, eig_sem.at[sem], {"row": to, "col": col})
+
+    def eig_core(across, along, half):
+        what = piece(eig_cols, eig_place(across, along), half)
+        send(what, what, core_sem, {"row": row + 1 - 2 * core, "col": col})
+
+    def eig_wait(across, along, half, sem):
+        arrived(piece(eig_cols, eig_place(across, along), half), eig_sem.at[sem])
+
+    def psi_send(across, along, way, half, sem):
+        what = piece(psi_rows, psi_place(across, along), half)
+        to = psi_place(1, 0) if way is None else psi_place(0, way)
+        send(what, what, psi_sem.at[sem], {"row": row, "col": to})
+
+    def psi_wait(across, along, half, sem):
+        arrived(piece(psi_rows, psi_place(across, along), half), psi_sem.at[sem])
+
+    eig_cols[row] = eig_ref[...]
+    psi_rows[col] = psi_ref[...]
+    eig_send(0, 0, 1, None, 0)
+    eig_send(0, 0, -1, None, 1)
+    eig_send(0, 0, None, None, 2)
+    eig_core(0, 0, None)
+    psi_send(0, 0, None, None, 2)
+
+    @pl.when((pair == 0) & (ring > 0))
+    def _():
+        arrived(panel_in.at[row], panel_sem.at[0])
+
+    @pl.when(pair == 0)
+    def _():
+        to_peers(panel_in.at[row], panel_in.at[row], panel_sem.at[1])
+
+    a_plane[ring] = a_ref[...]
     vecs[...] = jnp.zeros_like(vecs)
     images[...] = jnp.zeros_like(images)
     spot = lax.broadcasted_iota(jnp.int32, (tiles, tile), 0)
     lane = lax.broadcasted_iota(jnp.int32, (tiles, tile), 1)
     positions = ((spot % halves) * rows + spot // halves) * tile + lane
     slot = lax.broadcasted_iota(jnp.int32, (8, tile), 1)
-    others = panel_in.at[pl.ds(0, rows - 1)]
-    pltpu.make_async_copy(others, others, panel_sem).wait()
+
+    @pl.when(pair == 0)
+    def _():
+        arrived(panel_in.at[pl.ds(0, rows - 1)], panel_sem.at[1])
+
+    @pl.when(pair > 0)
+    def _():
+        arrived(panel_in, panel_sem.at[1])
+
     for r in range(rows):
         panel[:, r * halves : (r + 1) * halves, :] = panel_in[r]
+    half_rows = height // 2
+    arrived(a_plane.at[below], ring_sem.at[0])
+    onward = a_plane.at[below, pl.ds(0, half_rows)]
+    send(onward, onward, ring_sem.at[2], around[0])
+    arrived(a_plane.at[above], ring_sem.at[1])
+    back = a_plane.at[above, pl.ds(half_rows, half_rows)]
+    send(back, back, ring_sem.at[3], around[1])
+    eig_wait(0, -1, None, 0)
+    eig_send(0, -1, 1, 0, 3)
+    eig_core(0, -1, None)
+    eig_wait(0, 1, None, 1)
+    eig_send(0, 1, -1, 1, 4)
+    eig_core(0, 1, None)
+    eig_wait(1, 0, None, 2)
+    eig_send(1, 0, 1, None, 5)
+    eig_send(1, 0, -1, None, 6)
+    eig_core(1, 0, None)
+    psi_send(0, 0, 1, None, 0)
+    psi_send(0, 0, -1, None, 1)
+    psi_wait(1, 0, None, 2)
+    psi_send(1, 0, 1, None, 5)
+    psi_send(1, 0, -1, None, 6)
+    across = lax.rem(ring + 2, turns)
+    arrived(a_plane.at[across, pl.ds(0, half_rows)], ring_sem.at[2])
+    arrived(a_plane.at[across, pl.ds(half_rows, half_rows)], ring_sem.at[3])
+
+    def background(step):
+        @pl.when(step == 0)
+        def _():
+            eig_wait(0, 2, 0, 3)
+            eig_core(0, 2, 0)
+            eig_wait(0, 2, 1, 4)
+            eig_core(0, 2, 1)
+            eig_wait(1, -1, None, 5)
+            eig_send(1, -1, 1, 0, 7)
+            eig_core(1, -1, None)
+            eig_wait(1, 1, None, 6)
+            eig_send(1, 1, -1, 1, 8)
+            eig_core(1, 1, None)
+
+        @pl.when(step == 2)
+        def _():
+            eig_wait(1, 2, 0, 7)
+            eig_core(1, 2, 0)
+            eig_wait(1, 2, 1, 8)
+            eig_core(1, 2, 1)
+            psi_wait(0, -1, None, 0)
+            psi_send(0, -1, 1, 0, 3)
+            psi_wait(0, 1, None, 1)
+            psi_send(0, 1, -1, 1, 4)
+
+        @pl.when(step == 4)
+        def _():
+            psi_wait(1, -1, None, 5)
+            psi_send(1, -1, 1, 0, 7)
+            psi_wait(1, 1, None, 6)
+            psi_send(1, 1, -1, 1, 8)
+
+        @pl.when(step == 7)
+        def _():
+            for half in range(2):
+                psi_wait(0, 2, half, 3 + half)
+                psi_wait(1, 2, half, 7 + half)
+            arrived(eig_cols.at[pl.ds(0, rows // 2)], core_sem)
+            rotated[...] = jnp.zeros_like(rotated)
+
+        @pl.when(step >= PB // 2)
+        def _():
+            per = rows // (PB // 2)
+            for k in range(per):
+                r = (step - PB // 2) * per + k
+                left = [
+                    psi_rows[:, :, pl.ds(pl.multiple_of((h * rows + r) * tile, tile), tile)]
+                    for h in range(halves)
+                ]
+                left = jnp.concatenate([x.reshape(-1, tile) for x in left], axis=1)
+                rotated[...] += jnp.dot(
+                    left, eig_cols[r], preferred_element_type=jnp.float32
+                )
 
     def total(x):
         return jnp.sum(x, axis=(0, 1), keepdims=True)
@@ -88,13 +261,13 @@
     def reflector(column, step):
         at = total(jnp.where(positions == step, column, 0.0))
         pivot = total(jnp.where(positions == step + 1, column, 0.0))
-        below = positions > step + 1
-        tail = total(jnp.where(below, column * column, 0.0))
+        under = positions > step + 1
+        tail = total(jnp.where(under, column * column, 0.0))
         length = jnp.sqrt(pivot * pivot + tail)
         beta = jnp.where(pivot >= 0.0, -length, length)
         tau = (beta - pivot) / beta
         vector = jnp.where(
-            positions == step + 1, 1.0, jnp.where(below, column / (pivot - beta), 0.0)
+            positions == step + 1, 1.0, jnp.where(under, column / (pivot - beta), 0.0)
         )
         return at, beta, tau, vector
 
@@ -104,16 +277,20 @@
         diagonal = jnp.where(slot == step, at, diagonal)
         offdiag = jnp.where(slot == step, beta, offdiag)
         vec[...] = vector
-        spread = [jnp.broadcast_to(vec[e : e + 1, :], (8, tile)) for e in range(tiles)]
+        spread = []
+        for y in range(turns):
+            for b in range(blocks):
+                t = b * cols + pair * turns + y
+                e = lax.rem(t, rows) * halves + lax.div(t, rows)
+                spread.append(jnp.broadcast_to(vec[pl.ds(e, 1), :], (8, tile)))
 
         def band(group, _):
             at_rows = pl.ds(pl.multiple_of(group * 8, 8), 8)
             sums = [jnp.zeros((8, tile), jnp.float32) for _ in range(4)]
-            for e in range(tiles):
-                t = (e % halves) * rows + e // halves
-                b = t // cols
-                block = a_ref[t % cols, at_rows, b * tile : (b + 1) * tile]
-                sums[e % 4] = sums[e % 4] + block * spread[e]
+            for y in range(turns):
+                for b in range(blocks):
+                    block = a_plane[y, at_rows, b * tile : (b + 1) * tile]
+                    sums[b] = sums[b] + block * spread[y * blocks + b]
             lanes_sum[at_rows, :] = (sums[0] + sums[1]) + (sums[2] + sums[3])
             return 0
 
@@ -126,8 +303,9 @@
             )
         for half in range(halves):
             parts_out[step, half : half + 1, :] = product[0:1, half * tile : (half + 1) * tile]
-        to_peers(parts_out.at[step], parts_in.at[step, row], parts_sem.at[step])
-        parts_in[step, row] = parts_out[step]
+        to_peers(parts_out.at[step], parts_in.at[step, pair * rows + row], parts_sem.at[step])
+        parts_in[step, pair * rows + row] = parts_out[step]
+        background(step)
         by_vecs = totals(vecs[...] * vector[None])
         by_images = totals(images[...] * vector[None])
         known = jnp.sum(vecs[...] * by_images + images[...] * by_vecs, axis=0)
@@ -137,10 +315,9 @@
         head_w = totals(jnp.where(here[None], images[...], 0.0))
         ahead = panel[following] - jnp.sum(vecs[...] * head_w + images[...] * head_v, axis=0)
         vecs[step] = vector
-        rest = parts_in.at[step, pl.ds(0, rows - 1)]
-        pltpu.make_async_copy(rest, rest, parts_sem.at[step]).wait()
+        arrived(parts_in.at[step, pl.ds(0, 2 * rows - 1)], parts_sem.at[step])
         for r in range(rows):
-            whole[r * halves : (r + 1) * halves, :] = parts_in[step, r]
+            whole[r * halves : (r + 1) * halves, :] = parts_in[step, r] + parts_in[step, rows + r]
         image = tau * (whole[...] - known)
         image = image - 0.5 * tau * total(image * vector) * vector
         images[step] = image
@@ -151,8 +328,12 @@
 
     nothing = jnp.zeros((8, tile), jnp.float32)
     _, diagonal, offdiag = lax.fori_loop(0, PB, advance, (panel[0], nothing, nothing))
-    diag_ref[...] = diagonal
-    off_ref[...] = offdiag
+    diag_ref[...] = diagonal[0:1, 0:PB]
+    off_ref[...] = offdiag[0:1, 0:PB]
+    depth = rotated.shape[0]
+    for b in range(blocks):
+        rotated_tiles[pl.ds(b, depth, stride=blocks), :] = rotated[:, b * tile : (b + 1) * tile]
+    rotated_ref[...] = rotated_tiles[...].astype(rotated_ref.dtype)
     left_v = [vecs[:, pl.ds(halves * row + h, 1), :].reshape(PB, tile) for h in range(halves)]
     left_w = [images[:, pl.ds(halves * row + h, 1), :].reshape(PB, tile) for h in range(halves)]
     for b in range(blocks):
@@ -168,35 +349,58 @@
                 precision=lax.Precision.HIGHEST,
                 preferred_element_type=jnp.float32,
             )
-            block = a_ref[col, h * tile : (h + 1) * tile, b * tile : (b + 1) * tile]
+            block = a_ref[h * tile : (h + 1) * tile, b * tile : (b + 1) * tile]
             updated_ref[pl.ds(h * tile * blocks + b, tile, stride=blocks), :] = block - change
 
-    def drain(_, carry):
-        pltpu.make_async_copy(parts_out.at[0], parts_out.at[0], send_sem).wait()
+
+    def sent(ref):
+        pltpu.make_async_copy(ref, ref, send_sem).wait()
+
+    @pl.when(col == 0)
+    def _():
+        sent(panel_in.at[pl.ds(0, len(around))])
+
+    @pl.when(pair == 0)
+    def _():
+        sent(panel_in.at[pl.ds(0, rows)])
+        sent(panel_in.at[pl.ds(0, rows - 1)])
+
+    for _ in range(3):
+        sent(a_ref)
+    sent(eig_cols.at[pl.ds(0, 7)])
+    sent(eig_cols.at[pl.ds(0, rows // 2)])
+    sent(psi_rows.at[pl.ds(0, 7)])
+
+    def drain(step, carry):
+        sent(parts_in.at[step, pl.ds(0, 2 * rows - 1)])
         return carry
 
-    for _ in peers:
-        pltpu.make_async_copy(panel_out, panel_out, send_sem).wait()
-    lax.fori_loop(0, PB * (rows - 1), drain, 0)
-
-
-def reduce_panel(a_rows, rows):
-    cols, height, width = a_rows.shape
+    lax.fori_loop(0, PB, drain, 0)
+
+
+def reduce_panel(block, psi, eigvec, rows, cols):
+    height, width = block.shape
     tile = 128
     halves = height // tile
     tiles = rows * halves
+    depth = cols * psi.shape[0]
     vmem = pl.BlockSpec(memory_space=pltpu.VMEM)
     return pl.pallas_call(
         panel_kernel,
         out_shape=(
             jax.ShapeDtypeStruct((height * width // tile, tile), jnp.float32),
-            jax.ShapeDtypeStruct((8, tile), jnp.float32),
-            jax.ShapeDtypeStruct((8, tile), jnp.float32),
+            jax.ShapeDtypeStruct((1, PB), jnp.float32),
+            jax.ShapeDtypeStruct((1, PB), jnp.float32),
+            jax.ShapeDtypeStruct((depth * width // tile, tile), psi.dtype),
         ),
-        in_specs=[vmem],
-        out_specs=(vmem, vmem, vmem),
+        in_specs=[vmem, vmem, vmem],
+        out_specs=(vmem, vmem, vmem, vmem),
         scratch_shapes=[
-            pltpu.VMEM((PB, halves, tile), jnp.float32),
+            pltpu.VMEM((cols, *psi.shape), psi.dtype),
+            pltpu.VMEM((rows, *eigvec.shape), eigvec.dtype),
+            pltpu.VMEM((depth, width), jnp.float32),
+            pltpu.VMEM((depth * width // tile, tile), jnp.float32),
+            pltpu.VMEM((cols // 2, height, width), jnp.float32),
             pltpu.VMEM((rows, PB, halves, tile), jnp.float32),
             pltpu.VMEM((PB, tiles, tile), jnp.float32),
             pltpu.VMEM((PB, tiles, tile), jnp.float32),
@@ -204,17 +408,21 @@
             pltpu.VMEM((tiles, tile), jnp.float32),
             pltpu.VMEM((height, tile), jnp.float32),
             pltpu.VMEM((PB, halves, tile), jnp.float32),
-            pltpu.VMEM((PB, rows, halves, tile), jnp.float32),
+            pltpu.VMEM((PB, 2 * rows, halves, tile), jnp.float32),
             pltpu.VMEM((tiles, tile), jnp.float32),
             pltpu.SemaphoreType.DMA,
+            pltpu.SemaphoreType.DMA((4,)),
+            pltpu.SemaphoreType.DMA((2,)),
+            pltpu.SemaphoreType.DMA((PB,)),
+            pltpu.SemaphoreType.DMA((9,)),
             pltpu.SemaphoreType.DMA,
-            pltpu.SemaphoreType.DMA((PB,)),
+            pltpu.SemaphoreType.DMA((9,)),
         ],
         compiler_params=pltpu.CompilerParams(
             collective_id=0, has_side_effects=True, vmem_limit_bytes=48 * 1024 * 1024
         ),
         name="panel",
-    )(a_rows)
+    )(block, psi, eigvec)
 
 
 def lattice(row, col):
@@ -443,23 +651,20 @@
     row_count = lax.axis_size("row")
     col_count = lax.axis_size("col")
     reduced, correlation = reduce_front(psi, hpsi, row_count, col_count, row_tiles, col_tiles)
-    reduced, psi, eigvec = lax.optimization_barrier((reduced, psi, eigvec))
-    a_rows = lax.all_gather(reduced, "col")
-    psi_rows = lax.all_gather(psi, "col", axis=0, tiled=True)
-    rotation = lax.all_gather(eigvec, "row", axis=1, tiled=True)
-    updated, diagonal, offdiag = reduce_panel(a_rows, row_count)
-    rotated = jnp.dot(
-        psi_rows,
-        rotation.reshape(psi.shape[1], col_tiles * tile_size),
-        preferred_element_type=jnp.float32,
+    updated, diagonal, offdiag, rotated = reduce_panel(
+        reduced,
+        psi,
+        eigvec.reshape(row_tiles * tile_size, col_tiles * tile_size),
+        row_count,
+        col_count,
     )
     tile_shape = (row_tiles, 1, tile_size, col_tiles, 1, tile_size)
     return (
         correlation.reshape(tile_shape),
         updated.reshape(tile_shape),
-        diagonal[0, :PB],
-        offdiag[0, :PB],
-        rotated.astype(jnp.bfloat16).reshape(rotated.shape[0], col_tiles, 1, tile_size),
+        diagonal.reshape(PB),
+        offdiag.reshape(PB),
+        rotated.reshape(-1, col_tiles, 1, tile_size),
     )
 
 

time: 249 us -> 190 us (0.76)
  waiting for transfers between devices: 67.5 us -> 0 us
  Pallas kernels: 156 us -> 185 us
  between operations: 13.8 us -> 0.68 us
  matrix products: 4.07 us -> 0 us
  local copies, waits for them, and re-layouts: 6.95 us -> 4.4 us
    all_gather x3 -> x0, waiting for transfers between devices: 66.1 us -> none  [the longest x1 66.1 us: on_device(): a_rows = lax.all_gather(reduced, 'col')]
    pallas_call x1, Pallas kernels: 92.2 us -> 121 us  [reduce_panel(): pl.pallas_call(panel_kernel, out_shape=(jax.ShapeDtypeStruct((height * wi...]
    dot_general x1 -> x0, matrix products: 4.07 us -> none  [on_device(): jnp.dot(psi_rows, rotation.reshape(psi.shape[1], col_tiles * tile_size),...]
    unnamed x8 -> x10, local copies, waits for them, and re-layouts: 5.67 us -> 4.4 us
  transfers between devices with their start and end apart: 3 -> 0, of which waited for: 1 -> 0; matrix products, arithmetic and copies ran while one was open for 0% -> 0% of each run, Pallas kernels for 37% -> 0%
where the time goes in v3:
time: 190 us
  Pallas kernels  185 us (97%)
  local copies, waits for them, and re-layouts  4.4 us (2%)
    pallas_call x1, Pallas kernels, reduce_panel(): pl.pallas_call(panel_kernel, out_shape=(jax.ShapeDtypeStruct((height * wi...  121 us
    pallas_call x1, Pallas kernels, reduce_front(): pl.pallas_call(front_kernel, out_shape=(jax.ShapeDtypeStruct((height, wid...  63.6 us
    unnamed x10, local copies, waits for them, and re-layouts  4.4 us

profile of v3, /device:TPU:1, one launch (start us, length us, event | category | flops | bytes accessed | tf_op | source)
XLA Modules:
  0.0 189.9 jit_solution(16895510216399933332)
XLA Ops:
  0.6 0.0 copy-start
  0.6 0.0 copy-start.1
  0.7 1.0 copy.13
  1.7 0.0 copy-done
  1.7 0.0 copy-done.1
  1.7 63.6 %front.1 = (f32[256,512]{1,0:T(8,128)S(1)}, f32[1024,128]{1,0:T(8,128)S(1)}) custom-call(bf16[32,4096]{1,0:T(8,128)(2,1)S(1)} %copy-done, bf16[32,4096]{1,0:T(8,128)(2,1)S(1)} %copy-done.1), custom_call_target="tpu_custom_call" | custom-call | tf_op jit(solution)/shard_map/front/pallas_call | solution.py:624
  65.3 121.3 %panel.1 = (f32[1024,128]{1,0:T(8,128)S(1)}, f32[1,16]{1,0:T(1,128)S(1)}, f32[1,16]{1,0:T(1,128)S(1)}, bf16[1024,128]{1,0:T(8,128)(2,1)S(1)}) custom-call(f32[256,512]{1,0:T(8,128)S(1)} %get-tuple-element.12.a_ref, bf16[32,4096]{1,0:T(8,128)(2,1)S(1)} %copy-done, bf16[256,512]{1,0:T(8,128)(2,1)S(1)} %bitcast.17), custom_call_target="tpu_custom_call" | custom-call | tf_op jit(solution)/shard_map/panel/pallas_call | solution.py:388
  186.6 0.8 copy.19
  187.4 0.8 copy.20
  188.2 0.5 copy.21
  188.7 0.5 copy.22
  189.2 0.7 copy.23
Async XLA Ops:
  0.6 1.1 copy-start
  0.6 1.1 copy-start.1

commit v4 on v3

v4 whole, which is shorter than its diff:
```python
import jax
import jax.numpy as jnp
from jax import lax
from jax.experimental import pallas as pl
from jax.experimental.pallas import tpu as pltpu
from jax.sharding import PartitionSpec as P

PB = 16
MESH = pl.DeviceIdType.MESH


def split_three(x):
    high = x.astype(jnp.bfloat16)
    rest = x - high.astype(jnp.float32)
    mid = rest.astype(jnp.bfloat16)
    low = (rest - mid.astype(jnp.float32)).astype(jnp.bfloat16)
    return high, mid, low


def lattice(row, col):
    pair = {"row": lax.div(row, 8), "col": lax.div(col, 4)}
    ring = {"row": lax.rem(lax.div(row, 2), 4), "col": lax.rem(col, 4)}
    return pair, ring


def whole_kernel(
    psi_ref,
    hpsi_ref,
    eig_ref,
    corr_ref,
    updated_ref,
    diag_ref,
    off_ref,
    rotated_ref,
    by_row,
    by_col,
    total_s,
    a_ref,
    psi_rows,
    eig_cols,
    rotated,
    rotated_tiles,
    a_plane,
    panel_in,
    panel,
    vecs,
    images,
    vec,
    lanes_sum,
    parts_out,
    parts_in,
    whole,
    send_sem,
    swap_sem,
    gather_sem,
    gather_core,
    ring_sem,
    panel_sem,
    parts_sem,
    eig_sem,
    core_sem,
    psi_sem,
):
    rows = lax.axis_size("row")
    cols = lax.axis_size("col")
    row = lax.axis_index("row")
    col = lax.axis_index("col")
    tile = 128
    height, width = a_ref.shape
    halves, blocks = height // tile, width // tile
    tiles = rows * halves
    turns = cols // 2
    pairs, rings = lattice(row, col)
    pair, ring = pairs["col"], rings["col"]
    inputs = (psi_ref, hpsi_ref)
    core = lax.rem(row, 2)

    def place(axis, across, along):
        p = lax.rem(pairs[axis] + across, 2)
        q = lax.rem(rings[axis] + along + 4, 4)
        return p * 8 + q * 2 + core if axis == "row" else p * 4 + q

    order = sorted(
        ((d, e) for d in range(rows) for e in range(2) if d + e > 0),
        key=lambda de: -min(de[0], rows - de[0]) - 4 * de[1],
    )
    peers = [
        {"row": lax.rem(row + d, rows), "col": lax.rem(pair + e, 2) * turns + ring}
        for d, e in order
    ]
    around = [{"row": row, "col": pair * turns + lax.rem(ring + d, turns)} for d in (1, 3, 2)]
    beyond = [
        {"row": row, "col": (1 - pair) * turns + lax.rem(ring + d, turns)} for d in (1, 3, 2)
    ]
    row_order = sorted(range(1, rows), key=lambda d: -min(d, rows - d))
    row_peers = [lax.rem(row + d, rows) for d in row_order]
    col_peers = [lax.rem(col + d, cols) for d in range(1, cols)]
    greeted = peers + around + beyond
    barrier = pltpu.get_barrier_semaphore()
    for peer in greeted:
        pl.semaphore_signal(barrier, inc=1, device_id=peer, device_id_type=MESH)
    pl.semaphore_wait(barrier, len(greeted))

    def send(source, target, sem, where):
        pltpu.make_async_remote_copy(
            src_ref=source,
            dst_ref=target,
            send_sem=send_sem,
            recv_sem=sem,
            device_id={"row": row, "col": col, **where},
            device_id_type=MESH,
        ).start()

    def lanes(tile_index):
        return pl.ds(pl.multiple_of(tile_index * tile, tile), tile)

    def arrived(ref, sem):
        pltpu.make_async_copy(ref, ref, sem).wait()

    for n, source in enumerate(inputs):
        for r in row_peers:
            for h in range(halves):
                send(
                    source.at[:, lanes(h * rows + r)],
                    by_row.at[n, col, row, :, h * tile : (h + 1) * tile],
                    swap_sem.at[n, 0],
                    {"row": r},
                )
        for c in col_peers:
            for b in range(blocks):
                send(
                    source.at[:, lanes(b * cols + c)],
                    by_col.at[n, row, col, :, b * tile : (b + 1) * tile],
                    swap_sem.at[n, 1],
                    {"col": c},
                )
    for n, source in enumerate(inputs):
        for h in range(halves):
            by_row[n, col, row, :, h * tile : (h + 1) * tile] = source[:, lanes(h * rows + row)]
        for b in range(blocks):
            by_col[n, row, col, :, b * tile : (b + 1) * tile] = source[:, lanes(b * cols + col)]

    kinds = [(n, part) for n in range(2) for part in range(2)]
    axes = ("col", "row")
    held = (by_row, by_col)

    def gathered(n, part, across, along, half=None):
        whole = held[part].at[n, place(axes[part], across, along)]
        if half is None:
            return whole
        size = whole.shape[0] // 2
        return whole.at[pl.ds(half * size, size)]

    def along_ring(n, part, across, along, way, half, sem):
        what = gathered(n, part, across, along, half)
        where = {axes[part]: place(axes[part], 0, way)}
        send(what, what, gather_sem.at[n, part, sem], where)

    def to_core(n, part, across, along, half=None):
        if part == 1:
            what = gathered(n, part, across, along, half)
            send(what, what, gather_core.at[n], {"row": row + 1 - 2 * core})

    def wait_ring(n, part, across, along, half, sem):
        arrived(gathered(n, part, across, along, half), gather_sem.at[n, part, sem])

    for n, part in kinds:
        count = (rows if part == 0 else cols) - 1
        mine = (col if part == 0 else row,)
        arrived(held[part].at[n, mine[0], pl.ds(0, count)], swap_sem.at[n, part])
        along_ring(n, part, 0, 0, 1, None, 0)
        along_ring(n, part, 0, 0, -1, None, 1)
        what = gathered(n, part, 0, 0)
        send(what, what, gather_sem.at[n, part, 2], {axes[part]: place(axes[part], 1, 0)})
        to_core(n, part, 0, 0)
    for n, part in kinds:
        wait_ring(n, part, 0, -1, None, 0)
        along_ring(n, part, 0, -1, 1, 0, 3)
        to_core(n, part, 0, -1)
        wait_ring(n, part, 0, 1, None, 1)
        along_ring(n, part, 0, 1, -1, 1, 4)
        to_core(n, part, 0, 1)
        wait_ring(n, part, 1, 0, None, 2)
        along_ring(n, part, 1, 0, 1, None, 5)
        along_ring(n, part, 1, 0, -1, None, 6)
        to_core(n, part, 1, 0)
    for n, part in kinds:
        wait_ring(n, part, 0, 2, 0, 3)
        to_core(n, part, 0, 2, 0)
        wait_ring(n, part, 0, 2, 1, 4)
        to_core(n, part, 0, 2, 1)
        wait_ring(n, part, 1, -1, None, 5)
        along_ring(n, part, 1, -1, 1, 0, 7)
        to_core(n, part, 1, -1)
        wait_ring(n, part, 1, 1, None, 6)
        along_ring(n, part, 1, 1, -1, 1, 8)
        to_core(n, part, 1, 1)
    for n, part in kinds:
        wait_ring(n, part, 1, 2, 0, 7)
        to_core(n, part, 1, 2, 0)
        wait_ring(n, part, 1, 2, 1, 8)
        to_core(n, part, 1, 2, 1)
    for n in range(2):
        arrived(by_col.at[n, pl.ds(0, rows // 2)], gather_core.at[n])


    def eig_place(across, along):
        return place("row", across, along)

    def psi_place(across, along):
        return place("col", across, along)

    def piece(held, index, half):
        whole = held.at[index]
        if half is None:
            return whole
        size = whole.shape[0] // 2
        return whole.at[pl.ds(half * size, size)]

    def eig_send(across, along, way, half, sem):
        what = piece(eig_cols, eig_place(across, along), half)
        to = eig_place(1, 0) if way is None else eig_place(0, way)
        send(what, what, eig_sem.at[sem], {"row": to, "col": col})

    def eig_core(across, along, half):
        what = piece(eig_cols, eig_place(across, along), half)
        send(what, what, core_sem, {"row": row + 1 - 2 * core, "col": col})

    def eig_wait(across, along, half, sem):
        arrived(piece(eig_cols, eig_place(across, along), half), eig_sem.at[sem])

    def psi_send(across, along, way, half, sem):
        what = piece(psi_rows, psi_place(across, along), half)
        to = psi_place(1, 0) if way is None else psi_place(0, way)
        send(what, what, psi_sem.at[sem], {"row": row, "col": to})

    def psi_wait(across, along, half, sem):
        arrived(piece(psi_rows, psi_place(across, along), half), psi_sem.at[sem])

    eig_cols[row] = eig_ref[...]
    psi_rows[col] = psi_ref[...]
    eig_send(0, 0, 1, None, 0)
    eig_send(0, 0, -1, None, 1)
    eig_send(0, 0, None, None, 2)
    eig_core(0, 0, None)
    psi_send(0, 0, None, None, 2)


    depth = rows * by_row.shape[3]

    def row_block(n, c):
        return by_row[n, c].reshape(depth, halves * tile)

    def col_block(n, c):
        return by_col[n, :, c].reshape(depth, blocks * tile)

    def product(left, right):
        return lax.dot_general(
            left, right, (((0,), (0,)), ((), ())), preferred_element_type=jnp.float32
        )

    def add_s(c, carry):
        total_s[...] += product(row_block(0, c), col_block(0, c))
        return carry

    def add_a(c, carry):
        a_ref[...] += product(row_block(0, c), col_block(1, c)) + product(
            row_block(1, c), col_block(0, c)
        )
        return carry

    a_ref[...] = jnp.zeros_like(a_ref)
    lax.fori_loop(0, cols, add_a, 0)
    a_ref[...] = 0.5 * a_ref[...]

    def to_peers(source, target, recv):
        for peer in peers:
            send(source, target, recv, peer)

    @pl.when(col == 0)
    def _():
        for half in range(halves):
            first = a_ref[half * tile : (half + 1) * tile, 0:tile]
            panel_in[row, :, half, :] = jnp.transpose(first)[0:PB, :]
        for peer in around:
            send(panel_in.at[row], panel_in.at[row], panel_sem.at[0], peer)

    above, below = lax.rem(ring + 1, turns), lax.rem(ring + turns - 1, turns)
    half_rows = height // 2

    def part_of(where, half):
        return a_plane.at[where, pl.ds(half * half_rows, half_rows)]

    for half in range(2):
        for way, part in ((0, half), (1, 1 - half)):
            send(
                a_ref.at[pl.ds(part * half_rows, half_rows)],
                part_of(ring, part),
                ring_sem.at[2 * way + part],
                around[way],
            )


    @pl.when((pair == 0) & (ring > 0))
    def _():
        arrived(panel_in.at[row], panel_sem.at[0])

    @pl.when(pair == 0)
    def _():
        to_peers(panel_in.at[row], panel_in.at[row], panel_sem.at[1])

    a_plane[ring] = a_ref[...]
    vecs[...] = jnp.zeros_like(vecs)
    images[...] = jnp.zeros_like(images)
    spot = lax.broadcasted_iota(jnp.int32, (tiles, tile), 0)
    lane = lax.broadcasted_iota(jnp.int32, (tiles, tile), 1)
    positions = ((spot % halves) * rows + spot // halves) * tile + lane
    slot = lax.broadcasted_iota(jnp.int32, (8, tile), 1)

    @pl.when(pair == 0)
    def _():
        arrived(panel_in.at[pl.ds(0, rows - 1)], panel_sem.at[1])

    @pl.when(pair > 0)
    def _():
        arrived(panel_in, panel_sem.at[1])

    for r in range(rows):
        panel[:, r * halves : (r + 1) * halves, :] = panel_in[r]
    arrived(part_of(below, 0), ring_sem.at[0])
    send(part_of(below, 0), part_of(below, 0), ring_sem.at[4], around[0])
    arrived(part_of(above, 1), ring_sem.at[3])
    send(part_of(above, 1), part_of(above, 1), ring_sem.at[5], around[1])
    eig_wait(0, -1, None, 0)
    eig_send(0, -1, 1, 0, 3)
    eig_core(0, -1, None)
    eig_wait(0, 1, None, 1)
    eig_send(0, 1, -1, 1, 4)
    eig_core(0, 1, None)
    eig_wait(1, 0, None, 2)
    eig_send(1, 0, 1, None, 5)
    eig_send(1, 0, -1, None, 6)
    eig_core(1, 0, None)
    psi_send(0, 0, 1, None, 0)
    psi_send(0, 0, -1, None, 1)
    psi_wait(1, 0, None, 2)
    psi_send(1, 0, 1, None, 5)
    psi_send(1, 0, -1, None, 6)
    across = lax.rem(ring + 2, turns)
    arrived(part_of(below, 1), ring_sem.at[1])
    arrived(part_of(above, 0), ring_sem.at[2])
    arrived(part_of(across, 0), ring_sem.at[4])
    arrived(part_of(across, 1), ring_sem.at[5])

    def background(step):
        @pl.when(step == 0)
        def _():
            eig_wait(0, 2, 0, 3)
            eig_core(0, 2, 0)
            eig_wait(0, 2, 1, 4)
            eig_core(0, 2, 1)
            eig_wait(1, -1, None, 5)
            eig_send(1, -1, 1, 0, 7)
            eig_core(1, -1, None)
            eig_wait(1, 1, None, 6)
            eig_send(1, 1, -1, 1, 8)
            eig_core(1, 1, None)

        @pl.when(step == 2)
        def _():
            eig_wait(1, 2, 0, 7)
            eig_core(1, 2, 0)
            eig_wait(1, 2, 1, 8)
            eig_core(1, 2, 1)
            psi_wait(0, -1, None, 0)
            psi_send(0, -1, 1, 0, 3)
            psi_wait(0, 1, None, 1)
            psi_send(0, 1, -1, 1, 4)

        @pl.when(step == 3)
        def _():
            total_s[...] = jnp.zeros_like(total_s)
            lax.fori_loop(0, cols, add_s, 0)

        @pl.when(step == 5)
        def _():
            scale = 1.0 / (rows * cols * psi_ref.shape[0])
            for b in range(blocks):
                corr_ref[pl.ds(b, height, stride=blocks), :] = scale * total_s[
                    :, b * tile : (b + 1) * tile
                ]

        @pl.when(step == 4)
        def _():
            psi_wait(1, -1, None, 5)
            psi_send(1, -1, 1, 0, 7)
            psi_wait(1, 1, None, 6)
            psi_send(1, 1, -1, 1, 8)

        @pl.when(step == 6)
        def _():
            for half in range(2):
                psi_wait(0, 2, half, 3 + half)
                psi_wait(1, 2, half, 7 + half)
            arrived(eig_cols.at[pl.ds(0, rows // 2)], core_sem)
            rotated[...] = jnp.zeros_like(rotated)

        @pl.when((step >= PB // 2 - 1) & (step < PB - 1))
        def _():
            per = rows // (PB // 2)
            for k in range(per):
                r = (step - PB // 2 + 1) * per + k
                left = [
                    psi_rows[:, :, pl.ds(pl.multiple_of((h * rows + r) * tile, tile), tile)]
                    for h in range(halves)
                ]
                left = jnp.concatenate([x.reshape(-1, tile) for x in left], axis=1)
                rotated[...] += jnp.dot(left, eig_cols[r], preferred_element_type=jnp.float32)

        @pl.when(step == PB - 1)
        def _():
            depth = rotated.shape[0]
            for b in range(blocks):
                rotated_tiles[pl.ds(b, depth, stride=blocks), :] = rotated[
                    :, b * tile : (b + 1) * tile
                ]
            rotated_ref[...] = rotated_tiles[...].astype(rotated_ref.dtype)

    def total(x):
        return jnp.sum(x, axis=(0, 1), keepdims=True)

    def totals(x):
        return jnp.sum(x, axis=(1, 2), keepdims=True)

    def reflector(column, step):
        at = total(jnp.where(positions == step, column, 0.0))
        pivot = total(jnp.where(positions == step + 1, column, 0.0))
        under = positions > step + 1
        tail = total(jnp.where(under, column * column, 0.0))
        length = jnp.sqrt(pivot * pivot + tail)
        beta = jnp.where(pivot >= 0.0, -length, length)
        tau = (beta - pivot) / beta
        scale = 1.0 / (pivot - beta)
        vector = jnp.where(positions == step + 1, 1.0, jnp.where(under, column * scale, 0.0))
        return at, beta, tau, vector

    def advance(step, carry):
        column, diagonal, offdiag = carry
        at, beta, tau, vector = reflector(column, step)
        diagonal = jnp.where(slot == step, at, diagonal)
        offdiag = jnp.where(slot == step, beta, offdiag)
        vec[...] = vector
        spread = []
        for y in range(turns):
            for b in range(blocks):
                t = b * cols + pair * turns + y
                e = lax.rem(t, rows) * halves + lax.div(t, rows)
                spread.append(jnp.broadcast_to(vec[pl.ds(e, 1), :], (8, tile)))

        def band(group, _):
            at_rows = pl.ds(pl.multiple_of(group * 8, 8), 8)
            sums = [jnp.zeros((8, tile), jnp.float32) for _ in range(4)]
            for y in range(turns):
                for b in range(blocks):
                    block = a_plane[y, at_rows, b * tile : (b + 1) * tile]
                    sums[b] = sums[b] + block * spread[y * blocks + b]
            lanes_sum[at_rows, :] = (sums[0] + sums[1]) + (sums[2] + sums[3])
            return 0

        lax.fori_loop(0, height // 8, band, 0, unroll=4)
        ones = jnp.ones((16, tile), jnp.bfloat16)
        product = jnp.zeros((16, height), jnp.float32)
        for piece in split_three(lanes_sum[...]):
            product = product + lax.dot_general(
                ones, piece, (((1,), (1,)), ((), ())), preferred_element_type=jnp.float32
            )
        for half in range(halves):
            parts_out[step, half : half + 1, :] = product[0:1, half * tile : (half + 1) * tile]
        to_peers(parts_out.at[step], parts_in.at[step, pair * rows + row], parts_sem.at[step])
        parts_in[step, pair * rows + row] = parts_out[step]
        background(step)
        by_vecs = totals(vecs[...] * vector[None])
        by_images = totals(images[...] * vector[None])
        known = jnp.sum(vecs[...] * by_images + images[...] * by_vecs, axis=0)
        following = jnp.minimum(step + 1, PB - 1)
        here = positions == following
        head_v = totals(jnp.where(here[None], vecs[...], 0.0))
        head_w = totals(jnp.where(here[None], images[...], 0.0))
        ahead = panel[following] - jnp.sum(vecs[...] * head_w + images[...] * head_v, axis=0)
        vecs[step] = vector
        lead_v = total(jnp.where(here, vector, 0.0))
        half_tau = 0.5 * tau * tau
        arrived(parts_in.at[step, pl.ds(0, 2 * rows - 1)], parts_sem.at[step])
        for r in range(rows):
            whole[r * halves : (r + 1) * halves, :] = parts_in[step, r] + parts_in[step, rows + r]
        change = whole[...] - known
        along = half_tau * total(change * vector)
        lead_w = tau * total(jnp.where(here, change, 0.0)) - along * lead_v
        image = tau * change - along * vector
        images[step] = image
        column = ahead - vector * lead_w - image * lead_v
        return column, diagonal, offdiag

    nothing = jnp.zeros((8, tile), jnp.float32)
    _, diagonal, offdiag = lax.fori_loop(0, PB, advance, (panel[0], nothing, nothing))
    diag_ref[...] = diagonal[0:1, 0:PB]
    off_ref[...] = offdiag[0:1, 0:PB]
    left_v = [vecs[:, pl.ds(halves * row + h, 1), :].reshape(PB, tile) for h in range(halves)]
    left_w = [images[:, pl.ds(halves * row + h, 1), :].reshape(PB, tile) for h in range(halves)]
    for b in range(blocks):
        t = b * cols + col
        e = (t % rows) * halves + t // rows
        right_v = vecs[:, pl.ds(e, 1), :].reshape(PB, tile)
        right_w = images[:, pl.ds(e, 1), :].reshape(PB, tile)
        for h in range(halves):
            change = lax.dot_general(
                jnp.concatenate([left_v[h], left_w[h]], axis=0),
                jnp.concatenate([right_w, right_v], axis=0),
                (((0,), (0,)), ((), ())),
                precision=lax.Precision.HIGHEST,
                preferred_element_type=jnp.float32,
            )
            block = a_ref[h * tile : (h + 1) * tile, b * tile : (b + 1) * tile]
            updated_ref[pl.ds(h * tile * blocks + b, tile, stride=blocks), :] = block - change


    def sent(ref):
        pltpu.make_async_copy(ref, ref, send_sem).wait()

    @pl.when(col == 0)
    def _():
        sent(panel_in.at[pl.ds(0, len(around))])

    @pl.when(pair == 0)
    def _():
        sent(panel_in.at[pl.ds(0, rows)])
        sent(panel_in.at[pl.ds(0, rows - 1)])

    for _ in range(3):
        sent(a_ref)
    sent(eig_cols.at[pl.ds(0, 7)])
    sent(eig_cols.at[pl.ds(0, rows // 2)])
    sent(psi_rows.at[pl.ds(0, 7)])

    def drain(step, carry):
        sent(parts_in.at[step, pl.ds(0, 2 * rows - 1)])
        return carry

    lax.fori_loop(0, PB, drain, 0)

    for n in range(2):
        sent(by_row.at[n, 0, pl.ds(0, rows - 1)])
        sent(by_col.at[n, 0, pl.ds(0, cols - 1)])
        sent(by_row.at[n, pl.ds(0, 7)])
        sent(by_col.at[n, pl.ds(0, 7)])
        sent(by_col.at[n, pl.ds(0, rows // 2)])


def reduce_and_rotate(psi, hpsi, eigvec, rows, cols):
    height, width = eigvec.shape
    tile = 128
    halves = height // tile
    tiles = rows * halves
    depth = cols * psi.shape[0]
    vmem = pl.BlockSpec(memory_space=pltpu.VMEM)
    block = pltpu.VMEM((height, width), jnp.float32)
    vectors = pltpu.VMEM((PB, tiles, tile), jnp.float32)
    laid = jax.ShapeDtypeStruct((height * width // tile, tile), jnp.float32)
    return pl.pallas_call(
        whole_kernel,
        out_shape=(
            laid,
            laid,
            jax.ShapeDtypeStruct((1, PB), jnp.float32),
            jax.ShapeDtypeStruct((1, PB), jnp.float32),
            jax.ShapeDtypeStruct((depth * width // tile, tile), psi.dtype),
        ),
        in_specs=[vmem] * 3,
        out_specs=(vmem,) * 5,
        scratch_shapes=[
            pltpu.VMEM((2, cols, rows, psi.shape[0], height), psi.dtype),
            pltpu.VMEM((2, rows, cols, psi.shape[0], width), psi.dtype),
            block,
            block,
            pltpu.VMEM((cols, *psi.shape), psi.dtype),
            pltpu.VMEM((rows, *eigvec.shape), eigvec.dtype),
            pltpu.VMEM((depth, width), jnp.float32),
            pltpu.VMEM((depth * width // tile, tile), jnp.float32),
            pltpu.VMEM((cols // 2, height, width), jnp.float32),
            pltpu.VMEM((rows, PB, halves, tile), jnp.float32),
            vectors,
            vectors,
            vectors,
            pltpu.VMEM((tiles, tile), jnp.float32),
            pltpu.VMEM((height, tile), jnp.float32),
            pltpu.VMEM((PB, halves, tile), jnp.float32),
            pltpu.VMEM((PB, 2 * rows, halves, tile), jnp.float32),
            pltpu.VMEM((tiles, tile), jnp.float32),
            pltpu.SemaphoreType.DMA,
            pltpu.SemaphoreType.DMA((2, 2)),
            pltpu.SemaphoreType.DMA((2, 2, 9)),
            pltpu.SemaphoreType.DMA((2,)),
            pltpu.SemaphoreType.DMA((6,)),
            pltpu.SemaphoreType.DMA((2,)),
            pltpu.SemaphoreType.DMA((PB,)),
            pltpu.SemaphoreType.DMA((9,)),
            pltpu.SemaphoreType.DMA,
            pltpu.SemaphoreType.DMA((9,)),
        ],
        compiler_params=pltpu.CompilerParams(
            collective_id=0, has_side_effects=True, vmem_limit_bytes=56 * 1024 * 1024
        ),
        name="whole",
    )(psi, hpsi, eigvec)


def on_device(psi, hpsi, eigvec):
    row_tiles, _, tile_size, col_tiles = eigvec.shape[:4]
    correlation, updated, diagonal, offdiag, rotated = reduce_and_rotate(
        psi,
        hpsi,
        eigvec.reshape(row_tiles * tile_size, col_tiles * tile_size),
        lax.axis_size("row"),
        lax.axis_size("col"),
    )
    tile_shape = (row_tiles, 1, tile_size, col_tiles, 1, tile_size)
    return (
        correlation.reshape(tile_shape),
        updated.reshape(tile_shape),
        diagonal.reshape(PB),
        offdiag.reshape(PB),
        rotated.reshape(-1, col_tiles, 1, tile_size),
    )


def solution(mesh):
    return jax.shard_map(
        on_device,
        mesh=mesh,
        in_specs=(
            P(("row", "col"), None),
            P(("row", "col"), None),
            P(None, "row", None, None, "col", None),
        ),
        out_specs=(
            P(None, "row", None, None, "col", None),
            P(None, "row", None, None, "col", None),
            P(),
            P(),
            P("row", None, "col", None),
        ),
        check_vma=False,
    )
```

time: 190 us -> 182 us (0.958)
  Pallas kernels: 185 us -> 175 us
  local copies, waits for them, and re-layouts: 4.4 us -> 6.53 us
    pallas_call x2 -> x1, Pallas kernels: 185 us -> 175 us  [reduce_and_rotate(): pl.pallas_call(whole_kernel, out_shape=(laid, laid, jax.ShapeDtypeStruct(...]
    unnamed x10 -> x14, local copies, waits for them, and re-layouts: 4.4 us -> 6.53 us
where the time goes in v4:
time: 182 us
  Pallas kernels  175 us (96%)
  local copies, waits for them, and re-layouts  6.53 us (4%)
    pallas_call x1, Pallas kernels, reduce_and_rotate(): pl.pallas_call(whole_kernel, out_shape=(laid, laid, jax.ShapeDtypeStruct(...  175 us
    unnamed x14, local copies, waits for them, and re-layouts  6.53 us

profile of v4, /device:TPU:1, one launch (start us, length us, event | category | flops | bytes accessed | tf_op | source)
XLA Modules:
  0.0 182.2 jit_solution(17275373039663058983)
XLA Ops:
  0.6 1.7 copy.13
  2.3 175.1 %whole.1 = (f32[1024,128]{1,0:T(8,128)}, f32[1024,128]{1,0:T(8,128)}, f32[1,16]{1,0:T(1,128)}, f32[1,16]{1,0:T(1,128)}, bf16[1024,128]{1,0:T(8,128)(2,1)}) custom-call(bf16[32,4096]{1,0:T(8,128)(2,1)} %psi_ref.1, bf16[32,4096]{1,0:T(8,128)(2,1)} %hpsi_ref.1, bf16[256,512]{1,0:T(8,128)(2,1)} %bitcast.17), custom_call_target="tpu_custom_call" | custom-call | tf_op jit(solution)/shard_map/whole/pallas_call | solution.py:569
  177.4 0.0 copy-start
  177.4 2.3 %copy.19 = f32[2,1,128,4,1,128]{5,4,3,2,1,0:T(1,128)} copy(f32[2,1,128,4,1,128]{5,4,3,2,1,0:T(1,128)} %bitcast.19) | data formatting | bytes 1048576
  179.7 0.0 copy-done
  179.7 0.0 copy-start.3
  179.7 0.0 copy-start.1
  179.7 0.8 copy.20
  180.5 0.0 copy-done.3
  180.5 0.0 copy-start.2
  180.5 0.5 copy.21
  181.0 0.1 copy-done.2
  181.0 0.5 copy.22
  181.5 0.0 copy-done.1
  181.5 0.7 copy.23
Async XLA Ops:
  177.4 2.3 %copy-start = (f32[1024,128]{1,0:T(8,128)S(1)}, f32[1024,128]{1,0:T(8,128)}, u32[]{:S(2)}) copy-start(f32[1024,128]{1,0:T(8,128)} %get-tuple-element.11) | copy-start | bytes 1572868
  179.7 0.8 copy-start.3
  179.7 1.9 %copy-start.1 = (bf16[1024,128]{1,0:T(8,128)(2,1)S(1)}, bf16[1024,128]{1,0:T(8,128)(2,1)}, u32[]{:S(2)}) copy-start(bf16[1024,128]{1,0:T(8,128)(2,1)} %get-tuple-element.14) | copy-start | bytes 786436
  180.5 0.6 copy-start.2

commit v5 on v4

--- a/solution.py
+++ b/solution.py
@@ -237,15 +237,6 @@
     def psi_wait(across, along, half, sem):
         arrived(piece(psi_rows, psi_place(across, along), half), psi_sem.at[sem])
 
-    eig_cols[row] = eig_ref[...]
-    psi_rows[col] = psi_ref[...]
-    eig_send(0, 0, 1, None, 0)
-    eig_send(0, 0, -1, None, 1)
-    eig_send(0, 0, None, None, 2)
-    eig_core(0, 0, None)
-    psi_send(0, 0, None, None, 2)
-
-
     depth = rows * by_row.shape[3]
 
     def row_block(n, c):
@@ -308,6 +299,15 @@
     @pl.when(pair == 0)
     def _():
         to_peers(panel_in.at[row], panel_in.at[row], panel_sem.at[1])
+
+    eig_cols[row] = eig_ref[...]
+    psi_rows[col] = psi_ref[...]
+    eig_send(0, 0, 1, None, 0)
+    eig_send(0, 0, -1, None, 1)
+    eig_send(0, 0, None, None, 2)
+    eig_core(0, 0, None)
+    psi_send(0, 0, None, None, 2)
+
 
     a_plane[ring] = a_ref[...]
     vecs[...] = jnp.zeros_like(vecs)

time: 182 us -> 178 us (0.978)
  Pallas kernels: 175 us -> 170 us
    pallas_call x1, Pallas kernels: 175 us -> 170 us  [reduce_and_rotate(): pl.pallas_call(whole_kernel, out_shape=(laid, laid, jax.ShapeDtypeStruct(...]
where the time goes in v5:
time: 178 us; the launch traced here: 177 us
  Pallas kernels  170 us (96%)
  local copies, waits for them, and re-layouts  6.53 us (4%)
    pallas_call x1, Pallas kernels, reduce_and_rotate(): pl.pallas_call(whole_kernel, out_shape=(laid, laid, jax.ShapeDtypeStruct(...  170 us
    unnamed x14, local copies, waits for them, and re-layouts  6.53 us

profile of v5, /device:TPU:1, one launch (start us, length us, event | category | flops | bytes accessed | tf_op | source)
XLA Modules:
  0.0 177.5 jit_solution(13634318235908233556)
XLA Ops:
  0.6 1.7 copy.13
  2.3 170.3 %whole.1 = (f32[1024,128]{1,0:T(8,128)}, f32[1024,128]{1,0:T(8,128)}, f32[1,16]{1,0:T(1,128)}, f32[1,16]{1,0:T(1,128)}, bf16[1024,128]{1,0:T(8,128)(2,1)}) custom-call(bf16[32,4096]{1,0:T(8,128)(2,1)} %psi_ref.1, bf16[32,4096]{1,0:T(8,128)(2,1)} %hpsi_ref.1, bf16[256,512]{1,0:T(8,128)(2,1)} %bitcast.17), custom_call_target="tpu_custom_call" | custom-call | tf_op jit(solution)/shard_map/whole/pallas_call | solution.py:569
  172.6 0.0 copy-start
  172.6 2.3 %copy.19 = f32[2,1,128,4,1,128]{5,4,3,2,1,0:T(1,128)} copy(f32[2,1,128,4,1,128]{5,4,3,2,1,0:T(1,128)} %bitcast.19) | data formatting | bytes 1048576
  174.9 0.0 copy-done
  174.9 0.0 copy-start.3
  174.9 0.0 copy-start.1
  174.9 0.8 copy.20
  175.7 0.0 copy-done.3
  175.7 0.0 copy-start.2
  175.7 0.5 copy.21
  176.2 0.1 copy-done.2
  176.3 0.5 copy.22
  176.8 0.0 copy-done.1
  176.8 0.7 copy.23
Async XLA Ops:
  172.6 2.3 %copy-start = (f32[1024,128]{1,0:T(8,128)S(1)}, f32[1024,128]{1,0:T(8,128)}, u32[]{:S(2)}) copy-start(f32[1024,128]{1,0:T(8,128)} %get-tuple-element.11) | copy-start | bytes 1572868
  174.9 0.8 copy-start.3
  174.9 1.9 %copy-start.1 = (bf16[1024,128]{1,0:T(8,128)(2,1)S(1)}, bf16[1024,128]{1,0:T(8,128)(2,1)}, u32[]{:S(2)}) copy-start(bf16[1024,128]{1,0:T(8,128)(2,1)} %get-tuple-element.14) | copy-start | bytes 786436
  175.7 0.6 copy-start.2

commit v6 on v5

--- a/solution.py
+++ b/solution.py
@@ -50,6 +50,7 @@
     parts_out,
     parts_in,
     whole,
+    ends,
     send_sem,
     swap_sem,
     gather_sem,
@@ -60,6 +61,7 @@
     eig_sem,
     core_sem,
     psi_sem,
+    back_sem,
 ):
     rows = lax.axis_size("row")
     cols = lax.axis_size("col")
@@ -95,7 +97,19 @@
     row_order = sorted(range(1, rows), key=lambda d: -min(d, rows - d))
     row_peers = [lax.rem(row + d, rows) for d in row_order]
     col_peers = [lax.rem(col + d, cols) for d in range(1, cols)]
-    greeted = peers + around + beyond
+    chip = lax.div(row, 2)
+    head = row - core + 1
+    hops = {(0, 0): 0, (1, 0): 1, (0, 1): 2, (1, 1): 1}
+    steps = [(x, z, e) for x in range(2) for z in range(4) for e in range(2) if x + z + e > 0]
+    heads = [
+        {
+            "row": lax.rem(pairs["row"] + x, 2) * 8 + lax.rem(rings["row"] + z, 4) * 2 + 1,
+            "col": lax.rem(pair + e, 2) * turns + ring,
+        }
+        for x, z, e in sorted(steps, key=lambda q: -hops[q[0], q[2]] - min(q[1], 4 - q[1]))
+    ]
+    aside = [{**peer, "row": row + 1 - 2 * core} for peer in around]
+    greeted = peers + around + beyond + aside
     barrier = pltpu.get_barrier_semaphore()
     for peer in greeted:
         pl.semaphore_signal(barrier, inc=1, device_id=peer, device_id_type=MESH)
@@ -264,8 +278,8 @@
     lax.fori_loop(0, cols, add_a, 0)
     a_ref[...] = 0.5 * a_ref[...]
 
-    def to_peers(source, target, recv):
-        for peer in peers:
+    def to_heads(source, target, recv):
+        for peer in heads:
             send(source, target, recv, peer)
 
     @pl.when(col == 0)
@@ -273,32 +287,46 @@
         for half in range(halves):
             first = a_ref[half * tile : (half + 1) * tile, 0:tile]
             panel_in[row, :, half, :] = jnp.transpose(first)[0:PB, :]
+        mine = panel_in.at[row]
         for peer in around:
-            send(panel_in.at[row], panel_in.at[row], panel_sem.at[0], peer)
+            send(mine, mine, panel_sem.at[core], {**peer, "row": head})
+
+        @pl.when(core == 0)
+        def _():
+            send(mine, mine, panel_sem.at[0], {"row": head})
 
     above, below = lax.rem(ring + 1, turns), lax.rem(ring + turns - 1, turns)
     half_rows = height // 2
 
-    def part_of(where, half):
-        return a_plane.at[where, pl.ds(half * half_rows, half_rows)]
+    def part_of(where, k, half):
+        first = pl.multiple_of(k * height + half * half_rows, half_rows)
+        return a_plane.at[where, pl.ds(first, half_rows)]
 
     for half in range(2):
         for way, part in ((0, half), (1, 1 - half)):
             send(
                 a_ref.at[pl.ds(part * half_rows, half_rows)],
-                part_of(ring, part),
-                ring_sem.at[2 * way + part],
-                around[way],
+                part_of(ring, core, part),
+                ring_sem.at[core, 2 * way + part],
+                {**around[way], "row": head},
             )
 
-
-    @pl.when((pair == 0) & (ring > 0))
-    def _():
-        arrived(panel_in.at[row], panel_sem.at[0])
-
-    @pl.when(pair == 0)
-    def _():
-        to_peers(panel_in.at[row], panel_in.at[row], panel_sem.at[1])
+    own_rows = pl.ds(pl.multiple_of(core * height, height), height)
+
+    @pl.when(core == 0)
+    def _():
+        send(a_ref, a_plane.at[ring, own_rows], back_sem.at[3], {"row": head})
+
+    @pl.when((core == 1) & (pair == 0))
+    def _():
+        arrived(panel_in.at[row - core], panel_sem.at[0])
+
+        @pl.when(ring > 0)
+        def _():
+            arrived(panel_in.at[row], panel_sem.at[1])
+
+        both = panel_in.at[pl.ds(row - core, 2)]
+        to_heads(both, both, panel_sem.at[2])
 
     eig_cols[row] = eig_ref[...]
     psi_rows[col] = psi_ref[...]
@@ -309,28 +337,33 @@
     psi_send(0, 0, None, None, 2)
 
 
-    a_plane[ring] = a_ref[...]
-    vecs[...] = jnp.zeros_like(vecs)
-    images[...] = jnp.zeros_like(images)
     spot = lax.broadcasted_iota(jnp.int32, (tiles, tile), 0)
     lane = lax.broadcasted_iota(jnp.int32, (tiles, tile), 1)
     positions = ((spot % halves) * rows + spot // halves) * tile + lane
     slot = lax.broadcasted_iota(jnp.int32, (8, tile), 1)
 
-    @pl.when(pair == 0)
-    def _():
-        arrived(panel_in.at[pl.ds(0, rows - 1)], panel_sem.at[1])
-
-    @pl.when(pair > 0)
-    def _():
-        arrived(panel_in, panel_sem.at[1])
-
-    for r in range(rows):
-        panel[:, r * halves : (r + 1) * halves, :] = panel_in[r]
-    arrived(part_of(below, 0), ring_sem.at[0])
-    send(part_of(below, 0), part_of(below, 0), ring_sem.at[4], around[0])
-    arrived(part_of(above, 1), ring_sem.at[3])
-    send(part_of(above, 1), part_of(above, 1), ring_sem.at[5], around[1])
+    @pl.when(core == 1)
+    def _():
+        a_plane[ring, height : 2 * height, :] = a_ref[...]
+        vecs[...] = jnp.zeros_like(vecs)
+        images[...] = jnp.zeros_like(images)
+
+        @pl.when(pair == 0)
+        def _():
+            arrived(panel_in.at[pl.ds(0, rows - 2)], panel_sem.at[2])
+
+        @pl.when(pair > 0)
+        def _():
+            arrived(panel_in, panel_sem.at[2])
+
+        for r in range(rows):
+            panel[:, r * halves : (r + 1) * halves, :] = panel_in[r]
+        for k in range(2):
+            arrived(part_of(below, k, 0), ring_sem.at[k, 0])
+            send(part_of(below, k, 0), part_of(below, k, 0), ring_sem.at[k, 4], around[0])
+            arrived(part_of(above, k, 1), ring_sem.at[k, 3])
+            send(part_of(above, k, 1), part_of(above, k, 1), ring_sem.at[k, 5], around[1])
+
     eig_wait(0, -1, None, 0)
     eig_send(0, -1, 1, 0, 3)
     eig_core(0, -1, None)
@@ -347,10 +380,6 @@
     psi_send(1, 0, 1, None, 5)
     psi_send(1, 0, -1, None, 6)
     across = lax.rem(ring + 2, turns)
-    arrived(part_of(below, 1), ring_sem.at[1])
-    arrived(part_of(above, 0), ring_sem.at[2])
-    arrived(part_of(across, 0), ring_sem.at[4])
-    arrived(part_of(across, 1), ring_sem.at[5])
 
     def background(step):
         @pl.when(step == 0)
@@ -467,17 +496,18 @@
             lanes_sum[at_rows, :] = (sums[0] + sums[1]) + (sums[2] + sums[3])
             return 0
 
-        lax.fori_loop(0, height // 8, band, 0, unroll=4)
+        lax.fori_loop(0, 2 * height // 8, band, 0, unroll=4)
         ones = jnp.ones((16, tile), jnp.bfloat16)
-        product = jnp.zeros((16, height), jnp.float32)
+        product = jnp.zeros((16, 2 * height), jnp.float32)
         for piece in split_three(lanes_sum[...]):
             product = product + lax.dot_general(
                 ones, piece, (((1,), (1,)), ((), ())), preferred_element_type=jnp.float32
             )
-        for half in range(halves):
-            parts_out[step, half : half + 1, :] = product[0:1, half * tile : (half + 1) * tile]
-        to_peers(parts_out.at[step], parts_in.at[step, pair * rows + row], parts_sem.at[step])
-        parts_in[step, pair * rows + row] = parts_out[step]
+        for q in range(2 * halves):
+            parts_out[step, q : q + 1, :] = product[0:1, q * tile : (q + 1) * tile]
+        mine = pair * (rows // 2) + chip
+        to_heads(parts_out.at[step], parts_in.at[step, mine], parts_sem.at[step])
+        parts_in[step, mine] = parts_out[step]
         background(step)
         by_vecs = totals(vecs[...] * vector[None])
         by_images = totals(images[...] * vector[None])
@@ -488,23 +518,50 @@
         head_w = totals(jnp.where(here[None], images[...], 0.0))
         ahead = panel[following] - jnp.sum(vecs[...] * head_w + images[...] * head_v, axis=0)
         vecs[step] = vector
+        send(vecs.at[step], vecs.at[step], back_sem.at[0], {"row": row - core})
         lead_v = total(jnp.where(here, vector, 0.0))
         half_tau = 0.5 * tau * tau
-        arrived(parts_in.at[step, pl.ds(0, 2 * rows - 1)], parts_sem.at[step])
-        for r in range(rows):
-            whole[r * halves : (r + 1) * halves, :] = parts_in[step, r] + parts_in[step, rows + r]
+        arrived(parts_in.at[step, pl.ds(0, rows - 1)], parts_sem.at[step])
+        for m in range(rows // 2):
+            whole[m * 2 * halves : (m + 1) * 2 * halves, :] = (
+                parts_in[step, m] + parts_in[step, rows // 2 + m]
+            )
         change = whole[...] - known
         along = half_tau * total(change * vector)
         lead_w = tau * total(jnp.where(here, change, 0.0)) - along * lead_v
         image = tau * change - along * vector
         images[step] = image
+        send(images.at[step], images.at[step], back_sem.at[1], {"row": row - core})
         column = ahead - vector * lead_w - image * lead_v
         return column, diagonal, offdiag
 
-    nothing = jnp.zeros((8, tile), jnp.float32)
-    _, diagonal, offdiag = lax.fori_loop(0, PB, advance, (panel[0], nothing, nothing))
-    diag_ref[...] = diagonal[0:1, 0:PB]
-    off_ref[...] = offdiag[0:1, 0:PB]
+    @pl.when(core == 1)
+    def _():
+        for k in range(2):
+            arrived(part_of(below, k, 1), ring_sem.at[k, 1])
+            arrived(part_of(above, k, 0), ring_sem.at[k, 2])
+            arrived(part_of(across, k, 0), ring_sem.at[k, 4])
+            arrived(part_of(across, k, 1), ring_sem.at[k, 5])
+        arrived(a_plane.at[ring, pl.ds(0, height)], back_sem.at[3])
+        nothing = jnp.zeros((8, tile), jnp.float32)
+        _, diagonal, offdiag = lax.fori_loop(0, PB, advance, (panel[0], nothing, nothing))
+        ends[0] = diagonal
+        ends[1] = offdiag
+        send(ends, ends, back_sem.at[2], {"row": row - core})
+
+    @pl.when(core == 0)
+    def _():
+        def wait_step(step, carry):
+            background(step)
+            return carry
+
+        lax.fori_loop(0, PB, wait_step, 0)
+        arrived(vecs, back_sem.at[0])
+        arrived(images, back_sem.at[1])
+        arrived(ends, back_sem.at[2])
+
+    diag_ref[...] = ends[0, 0:1, 0:PB]
+    off_ref[...] = ends[1, 0:1, 0:PB]
     left_v = [vecs[:, pl.ds(halves * row + h, 1), :].reshape(PB, tile) for h in range(halves)]
     left_w = [images[:, pl.ds(halves * row + h, 1), :].reshape(PB, tile) for h in range(halves)]
     for b in range(blocks):
@@ -531,22 +588,41 @@
     def _():
         sent(panel_in.at[pl.ds(0, len(around))])
 
-    @pl.when(pair == 0)
-    def _():
-        sent(panel_in.at[pl.ds(0, rows)])
-        sent(panel_in.at[pl.ds(0, rows - 1)])
-
-    for _ in range(3):
+    for _ in range(2):
         sent(a_ref)
+
+    @pl.when(core == 0)
+    def _():
+        sent(a_ref)
+
+        @pl.when(col == 0)
+        def _():
+            sent(panel_in.at[0])
+
+    @pl.when(core == 1)
+    def _():
+        @pl.when(pair == 0)
+        def _():
+            sent(panel_in)
+            sent(panel_in.at[pl.ds(0, rows - 2)])
+
+        for _ in range(2):
+            sent(a_ref)
+        sent(vecs)
+        sent(images)
+        sent(ends)
+
     sent(eig_cols.at[pl.ds(0, 7)])
     sent(eig_cols.at[pl.ds(0, rows // 2)])
     sent(psi_rows.at[pl.ds(0, 7)])
 
     def drain(step, carry):
-        sent(parts_in.at[step, pl.ds(0, 2 * rows - 1)])
+        sent(parts_in.at[step, pl.ds(0, rows - 1)])
         return carry
 
-    lax.fori_loop(0, PB, drain, 0)
+    @pl.when(core == 1)
+    def _():
+        lax.fori_loop(0, PB, drain, 0)
 
     for n in range(2):
         sent(by_row.at[n, 0, pl.ds(0, rows - 1)])
@@ -586,26 +662,28 @@
             pltpu.VMEM((rows, *eigvec.shape), eigvec.dtype),
             pltpu.VMEM((depth, width), jnp.float32),
             pltpu.VMEM((depth * width // tile, tile), jnp.float32),
-            pltpu.VMEM((cols // 2, height, width), jnp.float32),
+            pltpu.VMEM((cols // 2, 2 * height, width), jnp.float32),
             pltpu.VMEM((rows, PB, halves, tile), jnp.float32),
             vectors,
             vectors,
             vectors,
             pltpu.VMEM((tiles, tile), jnp.float32),
-            pltpu.VMEM((height, tile), jnp.float32),
-            pltpu.VMEM((PB, halves, tile), jnp.float32),
-            pltpu.VMEM((PB, 2 * rows, halves, tile), jnp.float32),
+            pltpu.VMEM((2 * height, tile), jnp.float32),
+            pltpu.VMEM((PB, 2 * halves, tile), jnp.float32),
+            pltpu.VMEM((PB, rows, 2 * halves, tile), jnp.float32),
             pltpu.VMEM((tiles, tile), jnp.float32),
+            pltpu.VMEM((2, 8, tile), jnp.float32),
             pltpu.SemaphoreType.DMA,
             pltpu.SemaphoreType.DMA((2, 2)),
             pltpu.SemaphoreType.DMA((2, 2, 9)),
             pltpu.SemaphoreType.DMA((2,)),
-            pltpu.SemaphoreType.DMA((6,)),
-            pltpu.SemaphoreType.DMA((2,)),
+            pltpu.SemaphoreType.DMA((2, 6)),
+            pltpu.SemaphoreType.DMA((3,)),
             pltpu.SemaphoreType.DMA((PB,)),
             pltpu.SemaphoreType.DMA((9,)),
             pltpu.SemaphoreType.DMA,
             pltpu.SemaphoreType.DMA((9,)),
+            pltpu.SemaphoreType.DMA((4,)),
         ],
         compiler_params=pltpu.CompilerParams(
             collective_id=0, has_side_effects=True, vmem_limit_bytes=56 * 1024 * 1024

time: 178 us -> 172 us (0.966)
  Pallas kernels: 170 us -> 165 us
    pallas_call x1, Pallas kernels: 170 us -> 165 us  [reduce_and_rotate(): pl.pallas_call(whole_kernel, out_shape=(laid, laid, jax.ShapeDtypeStruct(...]
where the time goes in v6:
time: 172 us
  Pallas kernels  165 us (96%)
  local copies, waits for them, and re-layouts  6.53 us (4%)
    pallas_call x1, Pallas kernels, reduce_and_rotate(): pl.pallas_call(whole_kernel, out_shape=(laid, laid, jax.ShapeDtypeStruct(...  165 us
    unnamed x14, local copies, waits for them, and re-layouts  6.53 us

profile of v6, /device:TPU:1, one launch (start us, length us, event | category | flops | bytes accessed | tf_op | source)
XLA Modules:
  0.0 171.8 jit_solution(3232371110014043458)
XLA Ops:
  0.6 1.7 copy.13
  2.3 164.6 %whole.1 = (f32[1024,128]{1,0:T(8,128)}, f32[1024,128]{1,0:T(8,128)}, f32[1,16]{1,0:T(1,128)}, f32[1,16]{1,0:T(1,128)}, bf16[1024,128]{1,0:T(8,128)(2,1)}) custom-call(bf16[32,4096]{1,0:T(8,128)(2,1)} %psi_ref.1, bf16[32,4096]{1,0:T(8,128)(2,1)} %hpsi_ref.1, bf16[256,512]{1,0:T(8,128)(2,1)} %bitcast.17), custom_call_target="tpu_custom_call" | custom-call | tf_op jit(solution)/shard_map/whole/pallas_call | solution.py:645
  166.9 0.0 copy-start
  167.0 2.3 %copy.19 = f32[2,1,128,4,1,128]{5,4,3,2,1,0:T(1,128)} copy(f32[2,1,128,4,1,128]{5,4,3,2,1,0:T(1,128)} %bitcast.19) | data formatting | bytes 1048576
  169.2 0.0 copy-done
  169.2 0.0 copy-start.3
  169.2 0.0 copy-start.1
  169.2 0.8 copy.20
  170.0 0.0 copy-done.3
  170.0 0.0 copy-start.2
  170.0 0.5 copy.21
  170.5 0.1 copy-done.2
  170.6 0.5 copy.22
  171.1 0.0 copy-done.1
  171.1 0.7 copy.23
Async XLA Ops:
  166.9 2.3 %copy-start = (f32[1024,128]{1,0:T(8,128)S(1)}, f32[1024,128]{1,0:T(8,128)}, u32[]{:S(2)}) copy-start(f32[1024,128]{1,0:T(8,128)} %get-tuple-element.11) | copy-start | bytes 1572868
  169.2 0.8 copy-start.3
  169.2 1.9 %copy-start.1 = (bf16[1024,128]{1,0:T(8,128)(2,1)S(1)}, bf16[1024,128]{1,0:T(8,128)(2,1)}, u32[]{:S(2)}) copy-start(bf16[1024,128]{1,0:T(8,128)(2,1)} %get-tuple-element.14) | copy-start | bytes 786436
  170.0 0.6 copy-start.2

commit v7 on v6

--- a/solution.py
+++ b/solution.py
@@ -286,7 +286,7 @@
     def _():
         for half in range(halves):
             first = a_ref[half * tile : (half + 1) * tile, 0:tile]
-            panel_in[row, :, half, :] = jnp.transpose(first)[0:PB, :]
+            panel_in[row, :, half, :] = jnp.transpose(first)[0 : PB + 1, :]
         mine = panel_in.at[row]
         for peer in around:
             send(mine, mine, panel_sem.at[core], {**peer, "row": head})
@@ -471,14 +471,11 @@
         tau = (beta - pivot) / beta
         scale = 1.0 / (pivot - beta)
         vector = jnp.where(positions == step + 1, 1.0, jnp.where(under, column * scale, 0.0))
-        return at, beta, tau, vector
+        return at, beta, tau, scale, vector
 
     def advance(step, carry):
         column, diagonal, offdiag = carry
-        at, beta, tau, vector = reflector(column, step)
-        diagonal = jnp.where(slot == step, at, diagonal)
-        offdiag = jnp.where(slot == step, beta, offdiag)
-        vec[...] = vector
+        vec[...] = jnp.where(positions > step + 1, column, 0.0)
         spread = []
         for y in range(turns):
             for b in range(blocks):
@@ -496,7 +493,7 @@
             lanes_sum[at_rows, :] = (sums[0] + sums[1]) + (sums[2] + sums[3])
             return 0
 
-        lax.fori_loop(0, 2 * height // 8, band, 0, unroll=4)
+        lax.fori_loop(0, 2 * height // 8, band, 0, unroll=16)
         ones = jnp.ones((16, tile), jnp.bfloat16)
         product = jnp.zeros((16, 2 * height), jnp.float32)
         for piece in split_three(lanes_sum[...]):
@@ -508,6 +505,9 @@
         mine = pair * (rows // 2) + chip
         to_heads(parts_out.at[step], parts_in.at[step, mine], parts_sem.at[step])
         parts_in[step, mine] = parts_out[step]
+        at, beta, tau, scale, vector = reflector(column, step)
+        diagonal = jnp.where(slot == step, at, diagonal)
+        offdiag = jnp.where(slot == step, beta, offdiag)
         background(step)
         by_vecs = totals(vecs[...] * vector[None])
         by_images = totals(images[...] * vector[None])
@@ -521,12 +521,13 @@
         send(vecs.at[step], vecs.at[step], back_sem.at[0], {"row": row - core})
         lead_v = total(jnp.where(here, vector, 0.0))
         half_tau = 0.5 * tau * tau
+        base = panel[step + 1] - known
         arrived(parts_in.at[step, pl.ds(0, rows - 1)], parts_sem.at[step])
         for m in range(rows // 2):
             whole[m * 2 * halves : (m + 1) * 2 * halves, :] = (
                 parts_in[step, m] + parts_in[step, rows // 2 + m]
             )
-        change = whole[...] - known
+        change = scale * whole[...] + base
         along = half_tau * total(change * vector)
         lead_w = tau * total(jnp.where(here, change, 0.0)) - along * lead_v
         image = tau * change - along * vector
@@ -663,8 +664,8 @@
             pltpu.VMEM((depth, width), jnp.float32),
             pltpu.VMEM((depth * width // tile, tile), jnp.float32),
             pltpu.VMEM((cols // 2, 2 * height, width), jnp.float32),
-            pltpu.VMEM((rows, PB, halves, tile), jnp.float32),
-            vectors,
+            pltpu.VMEM((rows, PB + 1, halves, tile), jnp.float32),
+            pltpu.VMEM((PB + 1, tiles, tile), jnp.float32),
             vectors,
             vectors,
             pltpu.VMEM((tiles, tile), jnp.float32),

time: 172 us -> 169 us (0.983)
  Pallas kernels: 165 us -> 162 us
    pallas_call x1, Pallas kernels: 165 us -> 162 us  [reduce_and_rotate(): pl.pallas_call(whole_kernel, out_shape=(laid, laid, jax.ShapeDtypeStruct(...]
where the time goes in v7:
time: 169 us
  Pallas kernels  162 us (96%)
  local copies, waits for them, and re-layouts  6.53 us (4%)
    pallas_call x1, Pallas kernels, reduce_and_rotate(): pl.pallas_call(whole_kernel, out_shape=(laid, laid, jax.ShapeDtypeStruct(...  162 us
    unnamed x14, local copies, waits for them, and re-layouts  6.53 us

profile of v7, /device:TPU:1, one launch (start us, length us, event | category | flops | bytes accessed | tf_op | source)
XLA Modules:
  0.0 169.0 jit_solution(13773304600355008623)
XLA Ops:
  0.6 1.7 %copy.13 = bf16[32,8,4,128]{3,1,2,0:T(8,128)(2,1)} copy(bf16[32,8,4,128]{3,2,1,0:T(4,128)(2,1)} %bitcast.20) | data formatting | bytes 524288
  2.3 161.8 %whole.1 = (f32[1024,128]{1,0:T(8,128)}, f32[1024,128]{1,0:T(8,128)}, f32[1,16]{1,0:T(1,128)}, f32[1,16]{1,0:T(1,128)}, bf16[1024,128]{1,0:T(8,128)(2,1)}) custom-call(bf16[32,4096]{1,0:T(8,128)(2,1)} %psi_ref.1, bf16[32,4096]{1,0:T(8,128)(2,1)} %hpsi_ref.1, bf16[256,512]{1,0:T(8,128)(2,1)} %bitcast.17), custom_call_target="tpu_custom_call" | custom-call | tf_op jit(solution)/shard_map/whole/pallas_call | solution.py:646
  164.2 0.0 copy-start
  164.2 2.3 %copy.19 = f32[2,1,128,4,1,128]{5,4,3,2,1,0:T(1,128)} copy(f32[2,1,128,4,1,128]{5,4,3,2,1,0:T(1,128)} %bitcast.19) | data formatting | bytes 1048576
  166.4 0.0 copy-done
  166.4 0.0 copy-start.3
  166.4 0.0 copy-start.1
  166.4 0.8 copy.20
  167.2 0.0 copy-done.3
  167.2 0.0 copy-start.2
  167.2 0.5 copy.21
  167.7 0.1 copy-done.2
  167.8 0.5 copy.22
  168.3 0.0 copy-done.1
  168.3 0.7 copy.23
Async XLA Ops:
  164.2 2.3 %copy-start = (f32[1024,128]{1,0:T(8,128)S(1)}, f32[1024,128]{1,0:T(8,128)}, u32[]{:S(2)}) copy-start(f32[1024,128]{1,0:T(8,128)} %get-tuple-element.11) | copy-start | bytes 1572868
  166.4 0.8 copy-start.3
  166.4 1.9 %copy-start.1 = (bf16[1024,128]{1,0:T(8,128)(2,1)S(1)}, bf16[1024,128]{1,0:T(8,128)(2,1)}, u32[]{:S(2)}) copy-start(bf16[1024,128]{1,0:T(8,128)(2,1)} %get-tuple-element.14) | copy-start | bytes 786436
  167.2 0.6 copy-start.2

commit v8 on v7

--- a/solution.py
+++ b/solution.py
@@ -493,15 +493,18 @@
             lanes_sum[at_rows, :] = (sums[0] + sums[1]) + (sums[2] + sums[3])
             return 0
 
-        lax.fori_loop(0, 2 * height // 8, band, 0, unroll=16)
         ones = jnp.ones((16, tile), jnp.bfloat16)
-        product = jnp.zeros((16, 2 * height), jnp.float32)
-        for piece in split_three(lanes_sum[...]):
-            product = product + lax.dot_general(
-                ones, piece, (((1,), (1,)), ((), ())), preferred_element_type=jnp.float32
-            )
-        for q in range(2 * halves):
-            parts_out[step, q : q + 1, :] = product[0:1, q * tile : (q + 1) * tile]
+        groups = height // 8
+        for k in range(2):
+            lax.fori_loop(k * groups, (k + 1) * groups, band, 0, unroll=groups)
+            product = jnp.zeros((16, height), jnp.float32)
+            for piece in split_three(lanes_sum[k * height : (k + 1) * height, :]):
+                product = product + lax.dot_general(
+                    ones, piece, (((1,), (1,)), ((), ())), preferred_element_type=jnp.float32
+                )
+            for half in range(halves):
+                q = k * halves + half
+                parts_out[step, q : q + 1, :] = product[0:1, half * tile : (half + 1) * tile]
         mine = pair * (rows // 2) + chip
         to_heads(parts_out.at[step], parts_in.at[step, mine], parts_sem.at[step])
         parts_in[step, mine] = parts_out[step]

time: 169 us -> 169 us (level)
  no operation moved by 1% of the time
where the time goes in v8:
time: 169 us; the launch traced here: 168 us
  Pallas kernels  161 us (95%)
  local copies, waits for them, and re-layouts  6.53 us (4%)
    pallas_call x1, Pallas kernels, reduce_and_rotate(): pl.pallas_call(whole_kernel, out_shape=(laid, laid, jax.ShapeDtypeStruct(...  161 us
    unnamed x14, local copies, waits for them, and re-layouts  6.53 us

profile of v8, /device:TPU:1, one launch (start us, length us, event | category | flops | bytes accessed | tf_op | source)
XLA Modules:
  0.0 168.3 jit_solution(4806730791026888587)
XLA Ops:
  0.6 1.7 %copy.13 = bf16[32,8,4,128]{3,1,2,0:T(8,128)(2,1)} copy(bf16[32,8,4,128]{3,2,1,0:T(4,128)(2,1)} %bitcast.20) | data formatting | bytes 524288
  2.3 161.2 %whole.1 = (f32[1024,128]{1,0:T(8,128)}, f32[1024,128]{1,0:T(8,128)}, f32[1,16]{1,0:T(1,128)}, f32[1,16]{1,0:T(1,128)}, bf16[1024,128]{1,0:T(8,128)(2,1)}) custom-call(bf16[32,4096]{1,0:T(8,128)(2,1)} %psi_ref.1, bf16[32,4096]{1,0:T(8,128)(2,1)} %hpsi_ref.1, bf16[256,512]{1,0:T(8,128)(2,1)} %bitcast.17), custom_call_target="tpu_custom_call" | custom-call | tf_op jit(solution)/shard_map/whole/pallas_call | solution.py:649
  163.5 0.0 copy-start
  163.5 2.3 %copy.19 = f32[2,1,128,4,1,128]{5,4,3,2,1,0:T(1,128)} copy(f32[2,1,128,4,1,128]{5,4,3,2,1,0:T(1,128)} %bitcast.19) | data formatting | bytes 1048576
  165.8 0.0 copy-done
  165.8 0.0 copy-start.3
  165.8 0.0 copy-start.1
  165.8 0.8 copy.20
  166.6 0.0 copy-done.3
  166.6 0.0 copy-start.2
  166.6 0.5 copy.21
  167.1 0.1 copy-done.2
  167.1 0.5 copy.22
  167.6 0.0 copy-done.1
  167.6 0.7 copy.23
Async XLA Ops:
  163.5 2.3 %copy-start = (f32[1024,128]{1,0:T(8,128)S(1)}, f32[1024,128]{1,0:T(8,128)}, u32[]{:S(2)}) copy-start(f32[1024,128]{1,0:T(8,128)} %get-tuple-element.11) | copy-start | bytes 1572868
  165.8 0.8 copy-start.3
  165.8 1.9 %copy-start.1 = (bf16[1024,128]{1,0:T(8,128)(2,1)S(1)}, bf16[1024,128]{1,0:T(8,128)(2,1)}, u32[]{:S(2)}) copy-start(bf16[1024,128]{1,0:T(8,128)(2,1)} %get-tuple-element.14) | copy-start | bytes 786436
  166.6 0.6 copy-start.2
